TPU v7x, 256 devices: a whole 4x4x8 slice. The times are simulated.
256 devices in a mesh: dom: 256 (over y, x, z, core).
Axes of the slice: x: 4, y: 4, z: 8, core: 2. Of those that a mesh axis runs over, the one named last changes fastest.
Arguments:
- right_side: float32 [8192, 16, 128], P('dom')
- band_blocks: float32 [8192, 5, 128, 128], P('dom'), as said below
- link_blocks: float32 [256, 6, 4, 128, 128], P('dom'), as said below
- link_rows: int32 [256, 6, 4], P('dom'), may hold values from 0 to 32, as said below
Outputs:
- solution: float32 [8192, 16, 128], P('dom')
- residual: float32 [8192, 16, 128], P('dom')
Inputs may be any that keep to these rules, and one draw needn't show every extreme that they name: `link_rows`: entries are a row of device d (0 to 31) or 32 for an unused slot. Slot s of interface j of device d is paired with slot s of interface j xor 1 of the device it faces, and is used exactly when that one is. Each interface uses its first 1 to 4 slots and no row twice; in every draw some interface uses all 4. link_blocks[d, j, s] is the transpose of link_blocks[e, j xor 1, s] for the device e that interface j of d faces; blocks of unused slots are zero. band_blocks[g, 2 + m] is the transpose of band_blocks[g + m, 2 - m]; blocks whose column falls outside the device are zero. A is symmetric with a positive diagonal that exceeds the sum of magnitudes of the rest of its row.
All inputs are finite; a program needn't handle non-finite values.
Results may differ from a plain program's by a relative error of at most 0.0003.
Values sent between devices are 32-bit elements; how exact they have to be, the bound alone decides.
A program may use at most 64 MiB of HBM per device.

v0:
```python
import functools

import jax
import jax.numpy as jnp
from jax import lax
from jax.sharding import Mesh
from jax.sharding import PartitionSpec as P

ITERS = 3
DOM = ("dom_0", "dom_1", "dom_2", "dom_3")


HIGHEST = lax.Precision.HIGHEST


def shifted(value, axis, by):
    peers = lax.axis_size(axis)
    return lax.ppermute(value, axis, [(i, (i + by) % peers) for i in range(peers)])


def over_axes(value, axes):
    return functools.reduce(lax.psum, axes, value)


def facing_offsets(dev_count):
    return (1, -1, dev_count // 16, -(dev_count // 16), dev_count // 4, -(dev_count // 4))


def gram_matrix(left, right):
    return jnp.einsum("nsi,nti->st", left, right, precision=HIGHEST)


def mix_columns(field, coeffs):
    return jnp.einsum("nsi,st->nti", field, coeffs, precision=HIGHEST)


def small_product(left, right):
    return jnp.dot(left, right, precision=HIGHEST)


def solve_gram(matrix, target):
    symmetric = 0.5 * (matrix + matrix.T)
    factor = jnp.linalg.cholesky(symmetric)
    return jax.scipy.linalg.cho_solve((factor, True), target)


def apply_operator(field, band_blocks, link_blocks, link_rows):
    block_rows = field.shape[0]
    offset_list = facing_offsets(lax.axis_size(DOM))
    picks = (
        link_rows[0][:, :, None] == jnp.arange(block_rows, dtype=jnp.int32)[None, None, :]
    ).astype(field.dtype)
    padded = jnp.pad(field, ((2, 2), (0, 0), (0, 0)))
    total = jnp.zeros_like(field)
    for band_slot in range(5):
        total = total + jnp.einsum(
            "rsj,rij->rsi",
            padded[band_slot : band_slot + block_rows],
            band_blocks[:, band_slot],
            precision=HIGHEST,
        )
    for facing in range(6):
        source = jnp.einsum("hr,rsi->hsi", picks[facing ^ 1], field, precision=HIGHEST)
        arrived = shifted(source, DOM, -offset_list[facing])
        contrib = jnp.einsum("hsj,hij->hsi", arrived, link_blocks[0, facing], precision=HIGHEST)
        total = total + jnp.einsum("hr,hsi->rsi", picks[facing], contrib, precision=HIGHEST)
    return total


def shards(right_side, band_blocks, link_blocks, link_rows):
    solution = jnp.zeros_like(right_side)
    residual = right_side
    width = residual.shape[1]
    direction = residual
    along = residual
    curvature = jnp.zeros((width, width), residual.dtype)
    squares = curvature
    for iteration in range(ITERS):
        image = apply_operator(residual, band_blocks, link_blocks, link_rows)
        if iteration > 0:
            cross_local = gram_matrix(direction, image)
        else:
            cross_local = jnp.zeros((width, width), residual.dtype)
        fresh, inner, cross = (
            over_axes(gram_matrix(residual, residual), DOM),
            over_axes(gram_matrix(residual, image), DOM),
            over_axes(cross_local, DOM),
        )
        if iteration == 0:
            direction = residual
            along = image
            curvature = inner
        else:
            beta = solve_gram(squares, fresh)
            curvature = (
                inner
                + small_product(cross.T, beta)
                + small_product(beta.T, cross)
                + small_product(beta.T, small_product(curvature, beta))
            )
            direction = residual + mix_columns(direction, beta)
            along = image + mix_columns(along, beta)
        squares = fresh
        alpha = solve_gram(curvature, squares)
        solution = solution + mix_columns(direction, alpha)
        residual = residual - mix_columns(along, alpha)
    return (solution, residual)


def solution(mesh):
    split = Mesh(mesh.devices.reshape(4, 4, 8, 2), ("dom_0", "dom_1", "dom_2", "dom_3"))
    in_specs = (
        P(DOM, None, None),
        P(DOM, None, None, None),
        P(DOM, None, None, None, None),
        P(DOM, None, None),
    )
    out_specs = (P(DOM, None, None), P(DOM, None, None))
    return jax.shard_map(
        shards, mesh=split, in_specs=in_specs, out_specs=out_specs, check_vma=False
    )
```

profile of v0, /device:TPU:1, one launch (start us, length us, event | category | flops | bytes accessed | tf_op | source)
XLA Modules:
  0.0 374.7 jit_solution(4142028026099592110)
XLA Ops:
  26.4 4.9 %fusion.22 = f32[32,16,128]{2,1,0:T(8,128)S(1)} fusion(f32[32,16,128]{2,1,0:T(8,128)S(1)} %copy-done, f32[32,5,128,128]{3,2,1,0:T(8,128)} %param.8), kind=kOutput, calls=%fused_computation.22 | convolution fusion | flops 97517568 | bytes 2621440 | tf_op jit(solution)/shard_map/rsj,rij->rsi/dot_general | solution.py:56
  31.3 4.9 %fusion.4 = f32[32,16,128]{2,1,0:T(8,128)S(1)} fusion(f32[32,16,128]{2,1,0:T(8,128)S(1)} %copy-done, f32[32,5,128,128]{3,2,1,0:T(8,128)} %param.8), kind=kOutput, calls=%fused_computation.4 | convolution fusion | flops 94371840 | bytes 2621440 | tf_op jit(solution)/shard_map/rsj,rij->rsi/dot_general | solution.py:56
  36.3 5.1 %fusion.48 = f32[32,16,128]{2,1,0:T(8,128)S(1)} fusion(f32[32,16,128]{2,1,0:T(8,128)S(1)} %fusion.16, f32[32,16,128]{2,1,0:T(8,128)S(1)} %fusion.22, f32[32,16,128]{2,1,0:T(8,128)S(1)} %copy-done, f32[32,5,128,128]{3,2,1,0:T(8,128)} %param.8), kind=kOutput, calls=%fused_computation.46 | convolution fusion | flops 94502912 | bytes 3145728 | tf_op jit(solution)/shard_map/rsj,rij->rsi/dot_general | solution.py:56
  47.6 5.3 %fusion.134 = f32[32,16,128]{2,1,0:T(8,128)S(1)} fusion(f32[32,16,128]{2,1,0:T(8,128)S(1)} %fusion.4, f32[32,16,128]{2,1,0:T(8,128)S(1)} %fusion.48, f32[32,16,128]{2,1,0:T(8,128)S(1)} %copy-done, f32[32,5,128,128]{3,2,1,0:T(8,128)} %param.8, f32[32,16,128]{2,0,1:T(8,128)S(1)} %fusion.257, f32[32,16,128]{2,0,1:T(8,128)S(1)} %fusion.259, ...), kind=kOutput, calls=%fused_computation.89 | convolution fusion | flops 98041856 | bytes 4718592 | tf_op jit(solution)/shard_map/rsj,rij->rsi/dot_general | solution.py:56
  53.4 10.8 %all-reduce.11 = (f32[16,16]{1,0:T(8,128)S(1)}, f32[16,16]{1,0:T(8,128)S(1)}) all-reduce(f32[16,16]{1,0:T(8,128)S(1)} %convolution_bitcast_fusion.16, f32[16,16]{1,0:T(8,128)S(1)} %convolution_bitcast_fusion.17), channel_id=1, replica_groups=mesh['dom_0'=4,'dom_1'=4,'dom_2'=8,'dom_3'=2] {'dom_0'}, use_global_device_ids=true, to_apply=%region_6.0 | all-reduce | flops 512 | bytes 4096 | tf_op jit(solution)/shard_map/psum | solution.py:22
  64.2 11.0 %all-reduce.8 = (f32[16,16]{1,0:T(8,128)S(1)}, f32[16,16]{1,0:T(8,128)S(1)}) all-reduce(f32[16,16]{1,0:T(8,128)S(1)} %get-tuple-element.26, f32[16,16]{1,0:T(8,128)S(1)} %get-tuple-element.27), channel_id=1, replica_groups=mesh['dom_0'=4,'dom_1'=4,'dom_2'=8,'dom_3'=2] {'dom_1'}, use_global_device_ids=true, to_apply=%region_7.0 | all-reduce | flops 512 | bytes 4096 | tf_op jit(solution)/shard_map/psum | solution.py:22
  75.2 31.2 %all-reduce.5 = (f32[16,16]{1,0:T(8,128)S(1)}, f32[16,16]{1,0:T(8,128)S(1)}) all-reduce(f32[16,16]{1,0:T(8,128)S(1)} %get-tuple-element.18, f32[16,16]{1,0:T(8,128)S(1)} %get-tuple-element.19), channel_id=1, replica_groups=mesh['dom_0'=4,'dom_1'=4,'dom_2'=8,'dom_3'=2] {'dom_2'}, use_global_device_ids=true, to_apply=%region_8.10 | all-reduce | flops 512 | bytes 4096 | tf_op jit(solution)/shard_map/psum | solution.py:22
  106.5 13.0 %all-reduce.14 = (f32[16,16]{1,0:T(8,128)S(1)}, f32[16,16]{1,0:T(8,128)S(1)}) all-reduce(f32[16,16]{1,0:T(8,128)S(1)} %get-tuple-element.10, f32[16,16]{1,0:T(8,128)S(1)} %get-tuple-element.11), channel_id=1, replica_groups=mesh['dom_0'=4,'dom_1'=4,'dom_2'=8,'dom_3'=2] {'dom_3'}, use_global_device_ids=true, to_apply=%region_9.11 | all-reduce | flops 512 | bytes 4096 | tf_op jit(solution)/shard_map/psum | solution.py:22
  129.5 5.7 %fusion.20 = f32[32,16,128]{2,1,0:T(8,128)} fusion(f32[32,16,128]{2,1,0:T(8,128)S(1)} %fusion.97, f32[32,5,128,128]{3,2,1,0:T(8,128)} %param.8), kind=kOutput, calls=%fused_computation.20 | convolution fusion | flops 97517568 | bytes 2621440 | tf_op jit(solution)/shard_map/rsj,rij->rsi/dot_general | solution.py:56
  136.8 5.7 %fusion.2 = f32[32,16,128]{2,1,0:T(8,128)} fusion(f32[32,16,128]{2,1,0:T(8,128)S(1)} %fusion.97, f32[32,5,128,128]{3,2,1,0:T(8,128)} %param.8), kind=kOutput, calls=%fused_computation.2 | convolution fusion | flops 94371840 | bytes 2621440 | tf_op jit(solution)/shard_map/rsj,rij->rsi/dot_general | solution.py:56
  155.1 5.7 %fusion.54 = f32[32,16,128]{2,1,0:T(8,128)} fusion(f32[32,16,128]{2,1,0:T(8,128)S(1)} %fusion.14, f32[32,16,128]{2,1,0:T(8,128)} %fusion.20, f32[32,16,128]{2,1,0:T(8,128)S(1)} %fusion.97, f32[32,5,128,128]{3,2,1,0:T(8,128)} %param.8), kind=kOutput, calls=%fused_computation.48 | convolution fusion | flops 94502912 | bytes 3145728 | tf_op jit(solution)/shard_map/rsj,rij->rsi/dot_general | solution.py:56
  168.1 5.3 %fusion.137 = f32[32,16,128]{2,1,0:T(8,128)S(1)} fusion(f32[32,16,128]{2,1,0:T(8,128)} %fusion.2, f32[32,16,128]{2,1,0:T(8,128)S(1)} %copy-done.6, f32[32,16,128]{2,1,0:T(8,128)S(1)} %fusion.97, f32[32,5,128,128]{3,2,1,0:T(8,128)} %param.8, f32[32,16,128]{2,0,1:T(8,128)S(1)} %fusion.245, f32[32,16,128]{2,0,1:T(8,128)S(1)} %fusion.247, ...), kind=kOutput, calls=%fused_computation.90 | convolution fusion | flops 98041856 | bytes 4718592 | tf_op jit(solution)/shard_map/rsj,rij->rsi/dot_general | solution.py:56
  174.3 11.0 %all-reduce.10 = (f32[16,16]{1,0:T(8,128)S(1)}, f32[16,16]{1,0:T(8,128)S(1)}, f32[16,16]{0,1:T(8,128)S(1)}) all-reduce(f32[16,16]{1,0:T(8,128)S(1)} %convolution_bitcast_fusion.13, f32[16,16]{1,0:T(8,128)S(1)} %convolution_bitcast_fusion.15, ...), channel_id=1, replica_groups=mesh['dom_0'=4,'dom_1'=4,'dom_2'=8,'dom_3'=2] {'dom_0'}, use_global_device_ids=true, to_apply=%region_18.21 | all-reduce | flops 768 | bytes 6144 | tf_op jit(solution)/shard_map/psum | solution.py:22
  185.3 10.9 %all-reduce.7 = (f32[16,16]{1,0:T(8,128)S(1)}, f32[16,16]{1,0:T(8,128)S(1)}, f32[16,16]{0,1:T(8,128)S(1)}) all-reduce(f32[16,16]{1,0:T(8,128)S(1)} %get-tuple-element.23, f32[16,16]{1,0:T(8,128)S(1)} %get-tuple-element.24, f32[16,16]{0,1:T(8,128)S(1)} %get-tuple-element.25), channel_id=1, replica_groups=mesh['dom_0'=4,'dom_1'=4,'dom_2'=8,'dom_3'=2] {'dom_1'}, use_global_device_ids=true, to_apply=%region_19.22 | all-reduce | flops 768 | bytes 6144 | tf_op jit(solution)/shard_map/psum | solution.py:22
  196.2 31.2 %all-reduce.4 = (f32[16,16]{1,0:T(8,128)S(1)}, f32[16,16]{1,0:T(8,128)S(1)}, f32[16,16]{0,1:T(8,128)S(1)}) all-reduce(f32[16,16]{1,0:T(8,128)S(1)} %get-tuple-element.15, f32[16,16]{1,0:T(8,128)S(1)} %get-tuple-element.16, f32[16,16]{0,1:T(8,128)S(1)} %get-tuple-element.17), channel_id=1, replica_groups=mesh['dom_0'=4,'dom_1'=4,'dom_2'=8,'dom_3'=2] {'dom_2'}, use_global_device_ids=true, to_apply=%region_20.23 | all-reduce | flops 768 | bytes 6144 | tf_op jit(solution)/shard_map/psum | solution.py:22
  227.5 13.2 %all-reduce.13 = (f32[16,16]{1,0:T(8,128)S(1)}, f32[16,16]{1,0:T(8,128)S(1)}, f32[16,16]{0,1:T(8,128)S(1)}) all-reduce(f32[16,16]{1,0:T(8,128)S(1)} %get-tuple-element.7, f32[16,16]{1,0:T(8,128)S(1)} %get-tuple-element.8, f32[16,16]{0,1:T(8,128)S(1)} %get-tuple-element.9), channel_id=1, replica_groups=mesh['dom_0'=4,'dom_1'=4,'dom_2'=8,'dom_3'=2] {'dom_3'}, use_global_device_ids=true, to_apply=%region_21.24 | all-reduce | flops 768 | bytes 6144 | tf_op jit(solution)/shard_map/psum | solution.py:22
  252.1 5.7 %fusion.18 = f32[32,16,128]{2,1,0:T(8,128)} fusion(f32[32,16,128]{2,1,0:T(8,128)S(1)} %fusion.94, f32[32,5,128,128]{3,2,1,0:T(8,128)} %param.8), kind=kOutput, calls=%fused_computation.18 | convolution fusion | flops 97517568 | bytes 2621440 | tf_op jit(solution)/shard_map/rsj,rij->rsi/dot_general | solution.py:56
  261.2 5.7 %fusion = f32[32,16,128]{2,1,0:T(8,128)} fusion(f32[32,16,128]{2,1,0:T(8,128)S(1)} %fusion.94, f32[32,5,128,128]{3,2,1,0:T(8,128)} %param.8), kind=kOutput, calls=%fused_computation | convolution fusion | flops 94371840 | bytes 2621440 | tf_op jit(solution)/shard_map/rsj,rij->rsi/dot_general | solution.py:56
  271.3 5.7 %fusion.60 = f32[32,16,128]{2,1,0:T(8,128)} fusion(f32[32,16,128]{2,1,0:T(8,128)S(1)} %fusion.12, f32[32,16,128]{2,1,0:T(8,128)} %fusion.18, f32[32,16,128]{2,1,0:T(8,128)S(1)} %fusion.94, f32[32,5,128,128]{3,2,1,0:T(8,128)} %param.8), kind=kOutput, calls=%fused_computation.50 | convolution fusion | flops 94502912 | bytes 3145728 | tf_op jit(solution)/shard_map/rsj,rij->rsi/dot_general | solution.py:56
  293.4 5.3 %fusion.140 = f32[32,16,128]{2,1,0:T(8,128)S(1)} fusion(f32[32,16,128]{2,1,0:T(8,128)S(1)} %copy-done.4, f32[32,16,128]{2,1,0:T(8,128)S(1)} %copy-done.5, f32[32,16,128]{2,1,0:T(8,128)S(1)} %fusion.94, f32[32,5,128,128]{3,2,1,0:T(8,128)} %param.8, f32[32,16,128]{2,0,1:T(8,128)S(1)} %fusion.233, f32[32,16,128]{2,0,1:T(8,128)S(1)} %fusion.235, ...), kind=kOutput, calls=%fused_computation.91 | convolution fusion | flops 98041856 | bytes 4718592 | tf_op jit(solution)/shard_map/rsj,rij->rsi/dot_general | solution.py:56
  299.7 11.0 %all-reduce.9 = (f32[16,16]{1,0:T(8,128)S(1)}, f32[16,16]{1,0:T(8,128)S(1)}, f32[16,16]{1,0:T(8,128)S(1)}) all-reduce(f32[16,16]{1,0:T(8,128)S(1)} %convolution_bitcast_fusion.10, f32[16,16]{1,0:T(8,128)S(1)} %convolution_bitcast_fusion.12, ...), channel_id=1, replica_groups=mesh['dom_0'=4,'dom_1'=4,'dom_2'=8,'dom_3'=2] {'dom_0'}, use_global_device_ids=true, to_apply=%region_30.33 | all-reduce | flops 768 | bytes 6144 | tf_op jit(solution)/shard_map/psum | solution.py:22
  310.6 12.5 %all-reduce.6 = (f32[16,16]{1,0:T(8,128)S(1)}, f32[16,16]{1,0:T(8,128)S(1)}, f32[16,16]{1,0:T(8,128)S(1)}) all-reduce(f32[16,16]{1,0:T(8,128)S(1)} %get-tuple-element.20, f32[16,16]{1,0:T(8,128)S(1)} %get-tuple-element.21, f32[16,16]{1,0:T(8,128)S(1)} %get-tuple-element.22), channel_id=1, replica_groups=mesh['dom_0'=4,'dom_1'=4,'dom_2'=8,'dom_3'=2] {'dom_1'}, use_global_device_ids=true, to_apply=%region_31.34 | all-reduce | flops 768 | bytes 6144 | tf_op jit(solution)/shard_map/psum | solution.py:22
  323.1 30.1 %all-reduce.3 = (f32[16,16]{1,0:T(8,128)S(1)}, f32[16,16]{1,0:T(8,128)S(1)}, f32[16,16]{1,0:T(8,128)S(1)}) all-reduce(f32[16,16]{1,0:T(8,128)S(1)} %get-tuple-element.12, f32[16,16]{1,0:T(8,128)S(1)} %get-tuple-element.13, f32[16,16]{1,0:T(8,128)S(1)} %get-tuple-element.14), channel_id=1, replica_groups=mesh['dom_0'=4,'dom_1'=4,'dom_2'=8,'dom_3'=2] {'dom_2'}, use_global_device_ids=true, to_apply=%region_32.35 | all-reduce | flops 768 | bytes 6144 | tf_op jit(solution)/shard_map/psum | solution.py:22
  353.1 12.7 %all-reduce.12 = (f32[16,16]{1,0:T(8,128)S(1)}, f32[16,16]{1,0:T(8,128)S(1)}, f32[16,16]{1,0:T(8,128)S(1)}) all-reduce(f32[16,16]{1,0:T(8,128)S(1)} %get-tuple-element.4, f32[16,16]{1,0:T(8,128)S(1)} %get-tuple-element.5, f32[16,16]{1,0:T(8,128)S(1)} %get-tuple-element.6), channel_id=1, replica_groups=mesh['dom_0'=4,'dom_1'=4,'dom_2'=8,'dom_3'=2] {'dom_3'}, use_global_device_ids=true, to_apply=%region_33.36 | all-reduce | flops 768 | bytes 6144 | tf_op jit(solution)/shard_map/psum | solution.py:22
  (207 shorter events, 109.7 us)
Async XLA Ops:
  0.6 20.8 %copy-start = (f32[32,16,128]{2,1,0:T(8,128)S(1)}, f32[32,16,128]{2,1,0:T(8,128)}, u32[]{:S(2)}) copy-start(f32[32,16,128]{2,1,0:T(8,128)} %param.7) | copy-start | bytes 786436
  2.8 39.1 %collective-permute-start.5 = (f32[4,16,128]{2,1,0:T(8,128)S(1)}, f32[4,16,128]{2,1,0:T(8,128)S(1)}, u32[]{:S(2)}, u32[]{:S(2)}) collective-permute-start(f32[4,16,128]{2,1,0:T(8,128)S(1)} %copy.60), channel_id=1, source_target_pairs={{0,64},{1,65},{2,66},{3,67},{4,68},{5,69},{6,70},{7,71},{8,72},{9,... | collective-permute-start | bytes 98312 | tf_op jit(solution)/shard_map/ppermute | solution.py:18
  6.2 37.0 %collective-permute-start.4 = (f32[4,16,128]{2,1,0:T(8,128)S(1)}, f32[4,16,128]{2,1,0:T(8,128)S(1)}, u32[]{:S(2)}, u32[]{:S(2)}) collective-permute-start(f32[4,16,128]{2,1,0:T(8,128)S(1)} %copy.58), channel_id=1, source_target_pairs={{0,192},{1,193},{2,194},{3,195},{4,196},{5,197},{6,198},{7,199},{8... | collective-permute-start | bytes 98312 | tf_op jit(solution)/shard_map/ppermute | solution.py:18
  8.9 35.1 %collective-permute-start.3 = (f32[4,16,128]{2,1,0:T(8,128)S(1)}, f32[4,16,128]{2,1,0:T(8,128)S(1)}, u32[]{:S(2)}, u32[]{:S(2)}) collective-permute-start(f32[4,16,128]{2,1,0:T(8,128)S(1)} %copy.56), channel_id=1, source_target_pairs={{0,16},{1,17},{2,18},{3,19},{4,20},{5,21},{6,22},{7,23},{8,24},{9,... | collective-permute-start | bytes 98312 | tf_op jit(solution)/shard_map/ppermute | solution.py:18
  11.5 33.5 %collective-permute-start.2 = (f32[4,16,128]{2,1,0:T(8,128)S(1)}, f32[4,16,128]{2,1,0:T(8,128)S(1)}, u32[]{:S(2)}, u32[]{:S(2)}) collective-permute-start(f32[4,16,128]{2,1,0:T(8,128)S(1)} %copy.54), channel_id=1, source_target_pairs={{0,240},{1,241},{2,242},{3,243},{4,244},{5,245},{6,246},{7,247},{8... | collective-permute-start | bytes 98312 | tf_op jit(solution)/shard_map/ppermute | solution.py:18
  16.3 29.5 %collective-permute-start.1 = (f32[4,16,128]{2,1,0:T(8,128)S(1)}, f32[4,16,128]{2,1,0:T(8,128)S(1)}, u32[]{:S(2)}, u32[]{:S(2)}) collective-permute-start(f32[4,16,128]{2,1,0:T(8,128)S(1)} %copy.52), channel_id=1, source_target_pairs={{0,1},{1,2},{2,3},{3,4},{4,5},{5,6},{6,7},{7,8},{8,9},{9,10},{10,1... | collective-permute-start | bytes 98312 | tf_op jit(solution)/shard_map/ppermute | solution.py:18
  36.3 6.0 %copy-start.1 = (f32[1,6,4,128,128]{4,3,2,1,0:T(8,128)S(1)}, f32[1,6,4,128,128]{4,3,2,1,0:T(8,128)}, u32[]{:S(2)}) copy-start(f32[1,6,4,128,128]{4,3,2,1,0:T(8,128)} %param.9) | copy-start | bytes 4718596
  41.8 4.9 %collective-permute-start = (f32[4,16,128]{2,1,0:T(8,128)S(1)}, f32[4,16,128]{2,1,0:T(8,128)S(1)}, u32[]{:S(2)}, u32[]{:S(2)}) collective-permute-start(f32[4,16,128]{2,1,0:T(8,128)S(1)} %copy.50), channel_id=1, source_target_pairs={{0,255},{1,0},{2,1},{3,2},{4,3},{5,4},{6,5},{7,6},{8,7},{9,8},{10,... | collective-permute-start | bytes 98312 | tf_op jit(solution)/shard_map/ppermute | solution.py:18
  143.3 19.4 %collective-permute-start.11 = (f32[4,16,128]{2,1,0:T(8,128)S(1)}, f32[4,16,128]{2,1,0:T(8,128)S(1)}, u32[]{:S(2)}, u32[]{:S(2)}) collective-permute-start(f32[4,16,128]{2,1,0:T(8,128)S(1)} %copy.75), channel_id=1, source_target_pairs={{0,64},{1,65},{2,66},{3,67},{4,68},{5,69},{6,70},{7,71},{8,72},{9,... | collective-permute-start | bytes 98312 | tf_op jit(solution)/shard_map/ppermute | solution.py:18
  143.8 19.8 %collective-permute-start.10 = (f32[4,16,128]{2,1,0:T(8,128)S(1)}, f32[4,16,128]{2,1,0:T(8,128)S(1)}, u32[]{:S(2)}, u32[]{:S(2)}) collective-permute-start(f32[4,16,128]{2,1,0:T(8,128)S(1)} %copy.73), channel_id=1, source_target_pairs={{0,192},{1,193},{2,194},{3,195},{4,196},{5,197},{6,198},{7,199},{8... | collective-permute-start | bytes 98312 | tf_op jit(solution)/shard_map/ppermute | solution.py:18
  146.0 18.4 %collective-permute-start.9 = (f32[4,16,128]{2,1,0:T(8,128)S(1)}, f32[4,16,128]{2,1,0:T(8,128)S(1)}, u32[]{:S(2)}, u32[]{:S(2)}) collective-permute-start(f32[4,16,128]{2,1,0:T(8,128)S(1)} %copy.71), channel_id=1, source_target_pairs={{0,16},{1,17},{2,18},{3,19},{4,20},{5,21},{6,22},{7,23},{8,24},{9,... | collective-permute-start | bytes 98312 | tf_op jit(solution)/shard_map/ppermute | solution.py:18
  146.4 18.9 %collective-permute-start.8 = (f32[4,16,128]{2,1,0:T(8,128)S(1)}, f32[4,16,128]{2,1,0:T(8,128)S(1)}, u32[]{:S(2)}, u32[]{:S(2)}) collective-permute-start(f32[4,16,128]{2,1,0:T(8,128)S(1)} %copy.69), channel_id=1, source_target_pairs={{0,240},{1,241},{2,242},{3,243},{4,244},{5,245},{6,246},{7,247},{8... | collective-permute-start | bytes 98312 | tf_op jit(solution)/shard_map/ppermute | solution.py:18
  150.8 15.4 %collective-permute-start.7 = (f32[4,16,128]{2,1,0:T(8,128)S(1)}, f32[4,16,128]{2,1,0:T(8,128)S(1)}, u32[]{:S(2)}, u32[]{:S(2)}) collective-permute-start(f32[4,16,128]{2,1,0:T(8,128)S(1)} %copy.67), channel_id=1, source_target_pairs={{0,1},{1,2},{2,3},{3,4},{4,5},{5,6},{6,7},{7,8},{8,9},{9,10},{10,1... | collective-permute-start | bytes 98312 | tf_op jit(solution)/shard_map/ppermute | solution.py:18
  162.7 4.5 %collective-permute-start.6 = (f32[4,16,128]{2,1,0:T(8,128)S(1)}, f32[4,16,128]{2,1,0:T(8,128)S(1)}, u32[]{:S(2)}, u32[]{:S(2)}) collective-permute-start(f32[4,16,128]{2,1,0:T(8,128)S(1)} %copy.65), channel_id=1, source_target_pairs={{0,255},{1,0},{2,1},{3,2},{4,3},{5,4},{6,5},{7,6},{8,7},{9,8},{10,... | collective-permute-start | bytes 98312 | tf_op jit(solution)/shard_map/ppermute | solution.py:18
  270.8 8.2 %copy-start.3 = (f32[4,16,128]{2,0,1:T(4,128)S(1)}, f32[4,16,128]{2,0,1:T(4,128)}, u32[]{:S(2)}) copy-start(f32[4,16,128]{2,0,1:T(4,128)} %fusion.199) | copy-start | bytes 98308
  270.8 10.7 %copy-start.2 = (f32[4,16,128]{2,0,1:T(4,128)S(1)}, f32[4,16,128]{2,0,1:T(4,128)}, u32[]{:S(2)}) copy-start(f32[4,16,128]{2,0,1:T(4,128)} %fusion.201) | copy-start | bytes 98308
  270.8 17.0 %collective-permute-start.17 = (f32[4,16,128]{2,1,0:T(8,128)S(1)}, f32[4,16,128]{2,1,0:T(8,128)S(1)}, u32[]{:S(2)}, u32[]{:S(2)}) collective-permute-start(f32[4,16,128]{2,1,0:T(8,128)S(1)} %copy.91), channel_id=1, source_target_pairs={{0,64},{1,65},{2,66},{3,67},{4,68},{5,69},{6,70},{7,71},{8,72},{9,... | collective-permute-start | bytes 98312 | tf_op jit(solution)/shard_map/ppermute | solution.py:18
  279.0 14.4 %copy-start.4 = (f32[32,16,128]{2,1,0:T(8,128)S(1)}, f32[32,16,128]{2,1,0:T(8,128)}, u32[]{:S(2)}) copy-start(f32[32,16,128]{2,1,0:T(8,128)} %fusion) | copy-start | bytes 786436
  279.0 14.4 %copy-start.5 = (f32[32,16,128]{2,1,0:T(8,128)S(1)}, f32[32,16,128]{2,1,0:T(8,128)}, u32[]{:S(2)}) copy-start(f32[32,16,128]{2,1,0:T(8,128)} %fusion.60) | copy-start | bytes 786436
  279.0 9.9 %collective-permute-start.16 = (f32[4,16,128]{2,1,0:T(8,128)S(1)}, f32[4,16,128]{2,1,0:T(8,128)S(1)}, u32[]{:S(2)}, u32[]{:S(2)}) collective-permute-start(f32[4,16,128]{2,1,0:T(8,128)S(1)} %copy.89), channel_id=1, source_target_pairs={{0,192},{1,193},{2,194},{3,195},{4,196},{5,197},{6,198},{7,199},{8... | collective-permute-start | bytes 98312 | tf_op jit(solution)/shard_map/ppermute | solution.py:18
  281.5 8.4 %collective-permute-start.15 = (f32[4,16,128]{2,1,0:T(8,128)S(1)}, f32[4,16,128]{2,1,0:T(8,128)S(1)}, u32[]{:S(2)}, u32[]{:S(2)}) collective-permute-start(f32[4,16,128]{2,1,0:T(8,128)S(1)} %copy.87), channel_id=1, source_target_pairs={{0,16},{1,17},{2,18},{3,19},{4,20},{5,21},{6,22},{7,23},{8,24},{9,... | collective-permute-start | bytes 98312 | tf_op jit(solution)/shard_map/ppermute | solution.py:18
  281.8 8.9 %collective-permute-start.14 = (f32[4,16,128]{2,1,0:T(8,128)S(1)}, f32[4,16,128]{2,1,0:T(8,128)S(1)}, u32[]{:S(2)}, u32[]{:S(2)}) collective-permute-start(f32[4,16,128]{2,1,0:T(8,128)S(1)} %copy.85), channel_id=1, source_target_pairs={{0,240},{1,241},{2,242},{3,243},{4,244},{5,245},{6,246},{7,247},{8... | collective-permute-start | bytes 98312 | tf_op jit(solution)/shard_map/ppermute | solution.py:18
  286.3 5.3 %collective-permute-start.13 = (f32[4,16,128]{2,1,0:T(8,128)S(1)}, f32[4,16,128]{2,1,0:T(8,128)S(1)}, u32[]{:S(2)}, u32[]{:S(2)}) collective-permute-start(f32[4,16,128]{2,1,0:T(8,128)S(1)} %copy.83), channel_id=1, source_target_pairs={{0,1},{1,2},{2,3},{3,4},{4,5},{5,6},{6,7},{7,8},{8,9},{9,10},{10,1... | collective-permute-start | bytes 98312 | tf_op jit(solution)/shard_map/ppermute | solution.py:18
  287.8 4.7 %collective-permute-start.12 = (f32[4,16,128]{2,1,0:T(8,128)S(1)}, f32[4,16,128]{2,1,0:T(8,128)S(1)}, u32[]{:S(2)}, u32[]{:S(2)}) collective-permute-start(f32[4,16,128]{2,1,0:T(8,128)S(1)} %copy.81), channel_id=1, source_target_pairs={{0,255},{1,0},{2,1},{3,2},{4,3},{5,4},{6,5},{7,6},{8,7},{9,8},{10,... | collective-permute-start | bytes 98312 | tf_op jit(solution)/shard_map/ppermute | solution.py:18
  (1 other events, 5.4 us)
where the time goes:
time: 380 us; the launch traced here: 375 us
  blocking collectives  199 us (52%)
  matrix products  120 us (32%)
  starting transfers between devices  32 us (8%)
  other arithmetic  20.2 us (5%)
    psum x12, blocking collectives, over_axes(): return functools.reduce(lax.psum, axes, value)  199 us
    dot_general x15, matrix products, apply_operator(): jnp.einsum('rsj,rij->rsi', padded[band_slot:band_slot + block_rows], band...  79.7 us
    ppermute x18, starting transfers between devices, shifted(): lax.ppermute(value, axis, [(i, (i + by) % peers) for i in range(peers)])  32 us
    dot_general x18, matrix products, apply_operator(): jnp.einsum('hr,rsi->hsi', picks[facing ^ 1], field, precision=HIGHEST)  12.3 us
    another operation x15, other arithmetic, solve_gram(): factor = jnp.linalg.cholesky(symmetric)  10.8 us
    another operation x10, other arithmetic, solve_gram(): return jax.scipy.linalg.cho_solve((factor, True), target)  9.35 us
    dot_general x18, matrix products, apply_operator(): jnp.einsum('hsj,hij->hsi', arrived, link_blocks[0, facing], precision=HIG...  9.08 us
  transfers between devices with their start and end apart: 18, of which 0 were waited for; matrix products, arithmetic and copies ran while one was open for 15% of the time, Pallas kernels for 0%

commit v1 on v0

v1 whole, which is shorter than its diff:
```python
import functools

import jax
import jax.numpy as jnp
from jax import lax
from jax.experimental import pallas as pl
from jax.experimental.pallas import tpu as pltpu
from jax.sharding import PartitionSpec as P

S = 16
BS = 128
W = 2 * BS
H = 4
MESH = pl.DeviceIdType.MESH
F32 = jnp.float32
BF16 = jnp.bfloat16


def dot(a, b):
    return jnp.dot(a, b, preferred_element_type=F32)


def dot_nt(a, b):
    return lax.dot_general(a, b, (((1,), (1,)), ((), ())), preferred_element_type=F32)


def split(x):
    hi = x.astype(BF16)
    return hi, (x - hi.astype(F32)).astype(BF16)


def halves(x):
    return x[:S] + x[S:]


def iota(shape, dim):
    return lax.broadcasted_iota(jnp.int32, shape, dim)


def eliminate(table, first, count):
    lane = iota((1, BS), 1)
    for k in range(count):
        col = table[:, first + k : first + k + 1]
        inverse = 1.0 / col[k : k + 1]
        row = table[k : k + 1] * inverse
        table = jnp.where(lane == first + k, col * inverse, table - col * row)
    return table


def kernel(
    n,
    zs,
    rhs,
    band,
    link,
    rows,
    x_out,
    r_out,
    v0,
    stage,
    lstage,
    tiles,
    links,
    vs,
    xs,
    vr,
    yb,
    w1,
    v2,
    inv,
    send,
    recv0,
    recv1,
    recv2,
    sig1,
    sig2,
    gra1,
    gra2,
    grb1,
    grb2,
    in_sem,
    band_sem,
    halo_send,
    halo_recv,
    s1,
    r1,
    s2,
    r2,
):
    block_rows = v0.shape[0]
    pairs = block_rows // 2
    group = n // zs
    me = lax.axis_index("dom")
    offsets = (1, n - 1, n // 16, n - n // 16, n // 4, n - n // 4)
    z = (me // 2) % zs
    rank = me // (2 * zs) * 2 + me % 2

    def plane_device(other):
        return other // 2 * (2 * zs) + z * 2 + other % 2

    def ring_device(other):
        return me - z * 2 + other * 2

    load_v = pltpu.make_async_copy(rhs, v0, in_sem.at[0])
    load_l = pltpu.make_async_copy(link.at[0], lstage, in_sem.at[1])
    load_v.start()
    load_l.start()

    def load_band(p):
        return pltpu.make_async_copy(band.at[pl.ds(2 * p, 2)], stage.at[pl.ds(2 * p, 2)], band_sem.at[p])

    @pl.loop(0, pairs)
    def _(p):
        load_band(p).start()

    barrier = pltpu.get_barrier_semaphore()
    for offset in offsets:
        pl.semaphore_signal(barrier, inc=1, device_id=((me + offset) % n,), device_id_type=MESH)

    @pl.loop(1, group)
    def _(i):
        pl.semaphore_signal(barrier, inc=1, device_id=(plane_device((rank + i) % group),), device_id_type=MESH)

    @pl.loop(1, zs)
    def _(i):
        pl.semaphore_signal(barrier, inc=1, device_id=(ring_device((z + i) % zs),), device_id_type=MESH)

    @pl.loop(0, block_rows)
    def _(g):
        for j in range(6):
            found = 0
            for s in range(H):
                found = jnp.where(rows[0, j, s] == g, s + 1, found)
            inv[g * 6 + j] = found

    zero_tile = jnp.zeros((6, S, BS), F32)
    for buffer in (recv0, recv1, recv2):
        buffer[:, 0] = zero_tile
    xs[:, pl.ds(0, W)] = jnp.zeros((2 * S, W), BF16)
    xs[:, pl.ds(W * (pairs + 1), W)] = jnp.zeros((2 * S, W), BF16)
    zero_block = jnp.zeros((BS, BS), BF16)

    @pl.loop(0, pairs)
    def _(q):
        for part in range(2):
            tiles[q + 1, pl.ds(part * 3 * W, BS), pl.ds(BS, BS)] = zero_block
            tiles[q + 1, pl.ds(part * 3 * W + 2 * W + BS, BS), pl.ds(0, BS)] = zero_block

    for part in range(2):
        tiles[1, pl.ds(part * 3 * W, W)] = jnp.zeros((W, W), BF16)
        tiles[pairs, pl.ds(part * 3 * W + 2 * W, W)] = jnp.zeros((W, W), BF16)

    def put(p, value, slots):
        hi, lo = split(value)
        both = jnp.concatenate([hi, lo], axis=0)
        xs[:, pl.ds(pl.multiple_of(W * (p + 1), W), W)] = both
        vr[2 * p] = both[:, :BS]
        vr[2 * p + 1] = both[:, BS:]
        if slots is not None:
            keep(p, slots, hi, lo)

    def keep(p, slot, hi, lo):
        lanes = pl.ds(pl.multiple_of(W * p, W), W)
        vs[pl.ds(S * slot, S), lanes] = hi
        vs[pl.ds(4 * S + S * slot, S), lanes] = lo

    def first_field(p):
        return jnp.concatenate([v0[2 * p], v0[2 * p + 1]], axis=1)

    load_v.wait()

    @pl.loop(0, pairs)
    def _(p):
        put(p, first_field(p), 0)

    load_l.wait()

    @pl.loop(0, 6)
    def _(j):
        for s in range(H):
            hi, lo = split(lstage[j, s])
            links[j, s, pl.ds(0, BS)] = hi
            links[j, s, pl.ds(BS, BS)] = lo

    def halo_copy(step, j):
        return pltpu.make_async_remote_copy(
            src_ref=send.at[step, j],
            dst_ref=(recv0, recv1, recv2)[step].at[j ^ 1, pl.ds(1, H)],
            send_sem=halo_send.at[step, j],
            recv_sem=halo_recv.at[step, j ^ 1],
            device_id=((me + offsets[j]) % n,),
            device_id_type=MESH,
        )

    def multiply_links(step, ready=None):
        for j in (2, 3, 4, 5, 0, 1):
            for s in range(H):
                mine = vr[jnp.minimum(rows[0, j, s], block_rows - 1)]
                send[step, j, s] = halves(dot(jnp.concatenate([mine, mine], axis=1), links[j, s]))
            if ready is None:
                halo_copy(step, j).start()

    multiply_links(0, ready=False)
    pl.semaphore_wait(barrier, 6 + group - 1 + zs - 1)
    for j in (2, 3, 4, 5, 0, 1):
        halo_copy(0, j).start()

    on_diagonal = iota((BS, BS), 0) == iota((BS, BS), 1)

    def split_pair(p, total):
        load_band(p).wait()
        for local in range(2):
            for slot in range(5):
                block = stage[2 * p + local, slot]
                if slot == 2:
                    total = total + jnp.sum(jnp.where(on_diagonal, block, 0.0), axis=0, keepdims=True)
                away = local + slot - 2
                q = away // 2
                hi, lo = split(block)
                at = (1 - q) * W + local * BS
                lanes = pl.ds((away % 2) * BS, BS)
                tiles[p + q + 1, pl.ds(at, BS), lanes] = hi
                tiles[p + q + 1, pl.ds(3 * W + at, BS), lanes] = lo
        return total

    diagonal = lax.fori_loop(0, pairs, split_pair, jnp.zeros((1, BS), F32))

    def plane_copy(which, buffer, i):
        other = (rank + i) % group
        return pltpu.make_async_remote_copy(
            src_ref=buffer.at[rank],
            dst_ref=buffer.at[rank],
            send_sem=s1.at[which, other],
            recv_sem=r1.at[which, rank],
            device_id=(plane_device(other),),
            device_id_type=MESH,
        )

    def ring_copy(which, buffer, i):
        other = (z + i) % zs
        return pltpu.make_async_remote_copy(
            src_ref=buffer.at[z],
            dst_ref=buffer.at[z],
            send_sem=s2.at[which, other],
            recv_sem=r2.at[which, z],
            device_id=(ring_device(other),),
            device_id_type=MESH,
        )

    def plane_start(which, buffer, value):
        buffer[rank] = value

        @pl.loop(1, group)
        def _(i):
            plane_copy(which, buffer, i).start()

    def plane_finish(which, buffer):
        @pl.loop(1, group)
        def _(i):
            other = (rank + i) % group
            pltpu.make_async_remote_copy(
                src_ref=buffer.at[other],
                dst_ref=buffer.at[other],
                send_sem=s1.at[which, other],
                recv_sem=r1.at[which, other],
                device_id=(plane_device(other),),
                device_id_type=MESH,
            ).wait_recv()

        return jnp.sum(buffer[...], axis=0)

    def ring_start(which, buffer, value):
        buffer[z] = value

        @pl.loop(1, zs)
        def _(i):
            ring_copy(which, buffer, i).start()

    def ring_finish(which, buffer):
        @pl.loop(1, zs)
        def _(i):
            other = (z + i) % zs
            pltpu.make_async_remote_copy(
                src_ref=buffer.at[other],
                dst_ref=buffer.at[other],
                send_sem=s2.at[which, other],
                recv_sem=r2.at[which, other],
                device_id=(ring_device(other),),
                device_id_type=MESH,
            ).wait_recv()

        return jnp.sum(buffer[...], axis=0)

    plane_start(0, sig1, diagonal * (1.0 / (block_rows * BS)))

    def band_product():
        def body(q, carry):
            lhs = xs[:, pl.ds(pl.multiple_of(W * q, W), 3 * W)]
            out = dot(lhs, tiles[q + 1, pl.ds(0, 3 * W)]) + dot(lhs, tiles[q + 1, pl.ds(3 * W, 3 * W)])
            yb[q] = halves(out)
            return carry

        lax.fori_loop(0, pairs, body, 0, unroll=True)

    def landed(buffer, p):
        def of_row(g):
            total = buffer[0, inv[g * 6]]
            for j in range(1, 6):
                total = total + buffer[j, inv[g * 6 + j]]
            return total

        return yb[p] + jnp.concatenate([of_row(2 * p), of_row(2 * p + 1)], axis=1)

    def wait_halo(step):
        for j in range(6):
            halo_copy(step, j).wait_recv()

    band_product()
    wait_halo(0)

    @pl.loop(0, pairs)
    def _(p):
        value = landed(recv0, p)
        w1[p] = value
        put(p, value, None)

    multiply_links(1)
    ring_start(0, sig2, plane_finish(0, sig1))
    band_product()
    wait_halo(1)
    sigma = jnp.sum(ring_finish(0, sig2), axis=1, keepdims=True) * (1.0 / n)
    scale = 1.0 / sigma

    @pl.loop(0, pairs)
    def _(p):
        first = w1[p]
        one = first * scale - first_field(p)
        keep(p, 1, *split(one))
        two = (landed(recv1, p) * scale - first) * scale - one
        v2[p] = two
        put(p, two, 2)

    multiply_links(2)
    low = vs[pl.ds(0, 3 * S)]
    high = vs[pl.ds(4 * S, 3 * S)]
    stack = jnp.concatenate([low, high], axis=0)
    grams = dot_nt(stack, stack)
    grams = grams[: 3 * S] + grams[3 * S :]
    grams = grams[:, : 3 * S] + grams[:, 3 * S :]

    def gram_of(a, b):
        return grams[S * a : S * a + S, S * b : S * b + S]

    packed = jnp.concatenate(
        [gram_of(0, 0), gram_of(0, 1), gram_of(1, 1), gram_of(1, 2), gram_of(2, 2), jnp.zeros((S, 3 * S), F32)], axis=1
    )
    plane_start(1, gra1, packed)
    band_product()
    wait_halo(2)

    @pl.loop(0, pairs)
    def _(p):
        value = landed(recv2, p) * scale - v2[p]
        keep(p, 3, *split(value))

    left = jnp.concatenate([vs[pl.ds(2 * S, S)], vs[pl.ds(6 * S, S)]], axis=0)
    right = jnp.concatenate([vs[pl.ds(3 * S, S)], vs[pl.ds(7 * S, S)]], axis=0)
    last = halves(dot_nt(left, right))
    last = last[:, :S] + last[:, S:]
    lane = iota((S, BS), 1)
    place = lane // S == iota((S, BS), 0) % 8
    spread = jnp.where(place, jnp.concatenate([last] * 8, axis=1), 0.0)
    plane_start(2, grb1, jnp.concatenate([jnp.sum(spread[:8], axis=0, keepdims=True), jnp.sum(spread[8:], axis=0, keepdims=True)], axis=0))
    ring_start(1, gra2, plane_finish(1, gra1))
    ring_start(2, grb2, plane_finish(2, grb1))
    moments = ring_finish(1, gra2)

    in_h = lane < 3 * S
    blocks = []
    for i in range(3):
        upper = pltpu.roll(moments, BS - S * (i + 1), 1)
        lower = moments if i == 0 else pltpu.roll(moments, BS - S * i, 1)
        blocks.append(jnp.where(in_h, upper + lower, 0.0))
    blocks.append(jnp.where(in_h, moments, 0.0))
    table = jnp.concatenate(blocks, axis=0)
    table = eliminate(table, 0, S)[S:]
    table = eliminate(table, S, S)[S:]
    late = ring_finish(2, grb2)
    spread = jnp.concatenate([jnp.broadcast_to(late[:1], (8, BS)), jnp.broadcast_to(late[1:], (8, BS))], axis=0)
    spread = jnp.where(place, spread, 0.0)
    for shift in (64, 32, 16):
        spread = spread + pltpu.roll(spread, shift, 1)
    spread = jnp.where((lane >= 2 * S) & (lane < 3 * S), spread, 0.0)
    table = jnp.concatenate([table[:S] + spread, table[S:]], axis=0)
    coeffs = eliminate(table, 2 * S, S)[S:]
    coeffs = jnp.where(in_h, coeffs, 0.0)

    of_x = coeffs * scale
    of_r = -(coeffs + pltpu.roll(coeffs, S, 1))
    both = jnp.concatenate([of_x, of_r], axis=0)
    both = both + pltpu.roll(both, 4 * S, 1)
    hi, lo = split(both)
    mixer = jnp.concatenate([hi, lo], axis=0)

    def mix(p, carry):
        out = dot(mixer, vs[:, pl.ds(pl.multiple_of(W * p, W), W)])
        out = out[: 2 * S] + out[2 * S :]
        for local in range(2):
            lanes = slice(BS * local, BS * local + BS)
            x_out[2 * p + local] = out[:S, lanes]
            r_out[2 * p + local] = v0[2 * p + local] + out[S:, lanes]
        return carry

    lax.fori_loop(0, pairs, mix, 0, unroll=True)

    for step in range(3):
        for j in range(6):
            halo_copy(step, j).wait_send()
    for which, plane, ring in ((0, sig1, sig2), (1, gra1, gra2), (2, grb1, grb2)):

        @pl.loop(1, group)
        def _(i):
            plane_copy(which, plane, i).wait_send()

        @pl.loop(1, zs)
        def _(i):
            ring_copy(which, ring, i).wait_send()


def solution(mesh):
    n = mesh.devices.size
    zs = max(n // 32, 2)
    group = n // zs

    def local(right_side, band_blocks, link_blocks, link_rows):
        block_rows = right_side.shape[0]
        pairs = block_rows // 2
        field = jax.ShapeDtypeStruct(right_side.shape, F32)
        vmem = pltpu.VMEM
        dma = pltpu.SemaphoreType.DMA
        hbm = pl.BlockSpec(memory_space=pl.ANY)
        return pl.pallas_call(
            functools.partial(kernel, n, zs),
            out_shape=(field, field),
            in_specs=[hbm, hbm, hbm, pl.BlockSpec(memory_space=pltpu.SMEM)],
            out_specs=(pl.BlockSpec(memory_space=pltpu.VMEM),) * 2,
            scratch_shapes=[
                vmem((block_rows, S, BS), F32),
                vmem((block_rows, 5, BS, BS), F32),
                vmem((6, H, BS, BS), F32),
                vmem((pairs + 2, 6 * W, W), BF16),
                vmem((6, H, W, BS), BF16),
                vmem((8 * S, W * pairs), BF16),
                vmem((2 * S, W * (pairs + 2)), BF16),
                vmem((block_rows, 2 * S, BS), BF16),
                vmem((pairs, S, W), F32),
                vmem((pairs, S, W), F32),
                vmem((pairs, S, W), F32),
                pltpu.SMEM((block_rows * 6,), jnp.int32),
                vmem((3, 6, H, S, BS), F32),
                vmem((6, H + 1, S, BS), F32),
                vmem((6, H + 1, S, BS), F32),
                vmem((6, H + 1, S, BS), F32),
                vmem((group, 1, BS), F32),
                vmem((zs, 1, BS), F32),
                vmem((group, S, BS), F32),
                vmem((zs, S, BS), F32),
                vmem((group, 2, BS), F32),
                vmem((zs, 2, BS), F32),
                dma((2,)),
                dma((pairs,)),
                dma((3, 6)),
                dma((3, 6)),
                dma((3, group)),
                dma((3, group)),
                dma((3, zs)),
                dma((3, zs)),
            ],
            compiler_params=pltpu.CompilerParams(
                collective_id=0, has_side_effects=True, vmem_limit_bytes=56 * 1024 * 1024
            ),
        )(right_side, band_blocks, link_blocks, link_rows)

    return jax.shard_map(
        local,
        mesh=mesh,
        in_specs=(P("dom", None, None), P("dom", None, None, None), P("dom", None, None, None, None), P("dom", None, None)),
        out_specs=(P("dom", None, None), P("dom", None, None)),
        check_vma=False,
    )
```

time: 380 us -> 51.5 us (0.14); the launches traced: 375 us -> 51.3 us
  blocking collectives: 199 us -> 0 us
  matrix products: 120 us -> 0 us
  Pallas kernels: 0 us -> 46 us
  starting transfers between devices: 32 us -> 0 us
  other arithmetic: 20.2 us -> 0 us
    psum x12 -> x0, blocking collectives: 199 us -> none  [over_axes(): return functools.reduce(lax.psum, axes, value)]
    dot_general x95 -> x0, matrix products: 118 us -> none  [the longest x15 79.7 us: apply_operator(): jnp.einsum('rsj,rij->rsi', padded[band_slot:band_slot + block_rows], band...]
    pallas_call x0 -> x1, Pallas kernels: none -> 46 us  [local(): pl.pallas_call(functools.partial(kernel, n, zs), out_shape=(field, field)...]
    ppermute x18 -> x0, starting transfers between devices: 32 us -> none  [shifted(): lax.ppermute(value, axis, [(i, (i + by) % peers) for i in range(peers)])]
    another operation x25 -> x0, other arithmetic: 20.1 us -> none  [the longest x15 10.8 us: solve_gram(): factor = jnp.linalg.cholesky(symmetric)]
    unnamed x14 -> x3, local copies, waits for them, and re-layouts: 0.03 us -> 4.69 us
  transfers between devices with their start and end apart: 18 -> 0, of which waited for: 0 -> 0; matrix products, arithmetic and copies ran while one was open for 15% -> 0% of each run, Pallas kernels for 0% -> 0%
where the time goes in v1:
time: 51.5 us; the launch traced here: 51.3 us
  Pallas kernels  46 us (89%)
  local copies, waits for them, and re-layouts  4.69 us (9%)
  between operations  0.64 us (1%)
    pallas_call x1, Pallas kernels, local(): pl.pallas_call(functools.partial(kernel, n, zs), out_shape=(field, field)...  46 us
    unnamed x3, local copies, waits for them, and re-layouts  4.69 us

profile of v1, /device:TPU:1, one launch (start us, length us, event | category | flops | bytes accessed | tf_op | source)
XLA Modules:
  0.0 51.3 jit_solution(14974571949318353038)
XLA Ops:
  0.6 1.4 %copy.6.rows = s32[1,6,4]{2,1,0:T(8,128)} copy(s32[1,6,4]{1,2,0:T(4,128)} %param.7) | data formatting | bytes 192 | tf_op args[3]
  2.0 46.0 %shard_map.59 = (f32[32,16,128]{2,1,0:T(8,128)}, f32[32,16,128]{2,1,0:T(8,128)}) custom-call(f32[32,16,128]{2,1,0:T(8,128)} %rhs.1, f32[32,5,128,128]{3,2,1,0:T(8,128)} %band.1, f32[1,6,4,128,128]{4,3,2,1,0:T(8,128)} %link.1, s32[1,6,4]{2,1,0:T(8,128)} %copy.6.rows), custom_call_target="tpu_custom_call" | custom-call | tf_op jit(solution)/shard_map/pallas_call | solution.py:442
  48.0 1.7 %copy.9 = f32[32,16,128]{2,1,0:T(8,128)} copy(f32[32,16,128]{2,1,0:T(8,128)} %get-tuple-element.4) | data formatting | bytes 524288
  49.6 1.7 %copy.10 = f32[32,16,128]{2,1,0:T(8,128)} copy(f32[32,16,128]{2,1,0:T(8,128)} %get-tuple-element.5) | data formatting | bytes 524288

commit v2 on v1

v2 whole, which is shorter than its diff:
```python
import functools

import jax
import jax.numpy as jnp
from jax import lax
from jax.experimental import pallas as pl
from jax.experimental.pallas import tpu as pltpu
from jax.sharding import PartitionSpec as P

S = 16
BS = 128
W = 2 * BS
H = 4
MESH = pl.DeviceIdType.MESH
F32 = jnp.float32
BF16 = jnp.bfloat16


def dot(a, b):
    return jnp.dot(a, b, preferred_element_type=F32)


def dot_nt(a, b):
    return lax.dot_general(a, b, (((1,), (1,)), ((), ())), preferred_element_type=F32)


def split(x):
    hi = x.astype(BF16)
    return hi, (x - hi.astype(F32)).astype(BF16)


def halves(x):
    return x[:S] + x[S:]


def iota(shape, dim):
    return lax.broadcasted_iota(jnp.int32, shape, dim)


def eliminate(table, first, count):
    lane = iota((1, BS), 1)
    for k in range(count):
        col = table[:, first + k : first + k + 1]
        inverse = 1.0 / col[k : k + 1]
        row = table[k : k + 1] * inverse
        table = jnp.where(lane == first + k, col * inverse, table - col * row)
    return table


def eliminate_columns(upper, lower):
    count = len(upper)
    for k in range(count):
        inverse = 1.0 / upper[k][k : k + 1]
        up, low = upper[k] * inverse, lower[k] * inverse
        for j in range(count):
            if j != k:
                factor = upper[j][k : k + 1]
                upper[j], lower[j] = upper[j] - up * factor, lower[j] - low * factor
        upper[k], lower[k] = up, low
    return lower


def pack(gram, place):
    spread = jnp.where(place, jnp.concatenate([gram] * 8, axis=1), 0.0)
    return jnp.concatenate(
        [jnp.sum(spread[:8], axis=0, keepdims=True), jnp.sum(spread[8:], axis=0, keepdims=True)], axis=0
    )


def widen(packed):
    return jnp.concatenate(
        [jnp.broadcast_to(packed[:1], (8, BS)), jnp.broadcast_to(packed[1:], (8, BS))], axis=0
    )


def unpack(packed, place):
    spread = jnp.where(place, widen(packed), 0.0)
    for shift in (64, 32, 16):
        spread = spread + pltpu.roll(spread, shift, 1)
    return spread


def kernel(
    n,
    zs,
    rhs,
    band,
    link,
    rows_in,
    x_out,
    r_out,
    rows,
    v0,
    stage,
    lstage,
    tiles,
    links,
    vs,
    xs,
    vr,
    yb,
    ys,
    w1,
    v2,
    inv,
    send,
    recv0,
    recv1,
    recv2,
    sig1,
    sig2,
    gra1,
    gra2,
    grb1,
    grb2,
    in_sem,
    band_sem,
    halo_send,
    halo_recv,
    s1,
    r1,
    s2,
    r2,
):
    block_rows = v0.shape[0]
    pairs = block_rows // 2
    group = n // zs
    me = lax.axis_index("dom")
    offsets = (1, n - 1, n // 16, n - n // 16, n // 4, n - n // 4)
    z = lax.rem(lax.div(me, 2), zs)
    rank = lax.div(me, 2 * zs) * 2 + lax.rem(me, 2)

    def plane_device(other):
        return lax.div(other, 2) * (2 * zs) + z * 2 + lax.rem(other, 2)

    def ring_device(other):
        return me - z * 2 + other * 2

    barrier = pltpu.get_barrier_semaphore()
    with jax.named_scope("signals"):
        for i in range(1, group):
            device = plane_device(lax.rem(rank + i, group))
            pl.semaphore_signal(barrier, inc=1, device_id=(device,), device_id_type=MESH)
        for i in range(1, zs):
            device = ring_device(lax.rem(z + i, zs))
            pl.semaphore_signal(barrier, inc=1, device_id=(device,), device_id_type=MESH)
        for offset in offsets:
            device = lax.rem(me + offset, n)
            pl.semaphore_signal(barrier, inc=1, device_id=(device,), device_id_type=MESH)

    load_r = pltpu.make_async_copy(rows_in, rows, in_sem.at[0])
    load_v = pltpu.make_async_copy(rhs, v0, in_sem.at[1])
    load_l = pltpu.make_async_copy(link.at[0], lstage, in_sem.at[2])
    load_d = pltpu.make_async_copy(band.at[:, 2], stage.at[:, 2], in_sem.at[3])

    def load_band(p, side):
        at = (pl.ds(2 * p, 2), pl.ds(3 * side, 2))
        return pltpu.make_async_copy(band.at[at], stage.at[at], band_sem.at[p, side])

    with jax.named_scope("starts"):
        load_r.start()
        load_v.start()
        load_l.start()
        load_d.start()
        for p in range(pairs):
            load_band(p, 0).start()
            load_band(p, 1).start()

    with jax.named_scope("zeros"):
        for buffer in (recv0, recv1, recv2):
            buffer[:, 0] = jnp.zeros((6, S, BS), F32)
        xs[:, pl.ds(0, W)] = jnp.zeros((2 * S, W), BF16)
        xs[:, pl.ds(W * (pairs + 1), W)] = jnp.zeros((2 * S, W), BF16)
        zero_block = jnp.zeros((BS, BS), BF16)

        @pl.loop(0, pairs)
        def _(q):
            for part in range(2):
                tiles[q + 1, pl.ds(part * 3 * W, BS), pl.ds(BS, BS)] = zero_block
                tiles[q + 1, pl.ds(part * 3 * W + 2 * W + BS, BS), pl.ds(0, BS)] = zero_block

        for part in range(2):
            tiles[1, pl.ds(part * 3 * W, W)] = jnp.zeros((W, W), BF16)
            tiles[pairs, pl.ds(part * 3 * W + 2 * W, W)] = jnp.zeros((W, W), BF16)

    def each_pair(body):
        def step(p, carry):
            body(p)
            return carry

        lax.fori_loop(0, pairs, step, 0, unroll=True)

    def put(p, value, slot):
        hi, lo = split(value)
        both = jnp.concatenate([hi, lo], axis=0)
        xs[:, pl.ds(pl.multiple_of(W * (p + 1), W), W)] = both
        vr[2 * p] = both[:, :BS]
        vr[2 * p + 1] = both[:, BS:]
        if slot is not None:
            keep(p, slot, hi, lo)

    def keep(p, slot, hi, lo):
        lanes = pl.ds(pl.multiple_of(W * p, W), W)
        vs[pl.ds(S * slot, S), lanes] = hi
        vs[pl.ds(4 * S + S * slot, S), lanes] = lo

    def first_field(p):
        return jnp.concatenate([v0[2 * p], v0[2 * p + 1]], axis=1)

    with jax.named_scope("inv"):
        load_r.wait()
        at = [[rows[0, s, j] for s in range(H)] for j in range(6)]

        @pl.loop(0, block_rows)
        def _(g):
            for j in range(6):
                found = 0
                for s in range(H):
                    found = jnp.where(at[j][s] == g, s + 1, found)
                inv[g * 6 + j] = found

    with jax.named_scope("load_v"):
        load_v.wait()
        each_pair(lambda p: put(p, first_field(p), 0))

    with jax.named_scope("load_l"):
        load_l.wait()
        for j in range(6):
            for s in range(H):
                hi, lo = split(lstage[j, s])
                links[j, s, pl.ds(0, BS)] = hi
                links[j, s, pl.ds(BS, BS)] = lo

    def halo_copy(step, j):
        return pltpu.make_async_remote_copy(
            src_ref=send.at[step, j],
            dst_ref=(recv0, recv1, recv2)[step].at[j ^ 1, pl.ds(1, H)],
            send_sem=halo_send.at[step, j],
            recv_sem=halo_recv.at[step, j ^ 1],
            device_id=(lax.rem(me + offsets[j], n),),
            device_id_type=MESH,
        )

    def row_of(j, s):
        return vr[jnp.minimum(rows[0, s, j], block_rows - 1)]

    def multiply_links(step):
        for j in range(6):
            for s in range(H):
                mine = row_of(j, s)
                send[step, j, s] = halves(dot(jnp.concatenate([mine, mine], axis=1), links[j, s]))

    def send_links(step):
        for j in (0, 1, 2, 3, 4, 5):
            halo_copy(step, j).start()

    with jax.named_scope("links0"):
        multiply_links(0)

    def plane_copy(which, buffer, i):
        other = lax.rem(rank + i, group)
        return pltpu.make_async_remote_copy(
            src_ref=buffer.at[rank],
            dst_ref=buffer.at[rank],
            send_sem=s1.at[which, other],
            recv_sem=r1.at[which, rank],
            device_id=(plane_device(other),),
            device_id_type=MESH,
        )

    def ring_copy(which, buffer, i):
        other = lax.rem(z + i, zs)
        return pltpu.make_async_remote_copy(
            src_ref=buffer.at[z],
            dst_ref=buffer.at[z],
            send_sem=s2.at[which, other],
            recv_sem=r2.at[which, z],
            device_id=(ring_device(other),),
            device_id_type=MESH,
        )

    def times(count, body):
        def step(i, carry):
            body(i)
            return carry

        lax.fori_loop(1, count, step, 0, unroll=True)

    def plane_start(which, buffer, value):
        buffer[rank] = value
        times(group, lambda i: plane_copy(which, buffer, i).start())

    def plane_finish(which, buffer):
        def wait(i):
            other = lax.rem(rank + i, group)
            pltpu.make_async_remote_copy(
                src_ref=buffer.at[other],
                dst_ref=buffer.at[other],
                send_sem=s1.at[which, other],
                recv_sem=r1.at[which, other],
                device_id=(plane_device(other),),
                device_id_type=MESH,
            ).wait_recv()

        times(group, wait)
        return jnp.sum(buffer[...], axis=0)

    def ring_start(which, buffer, value):
        buffer[z] = value
        times(zs, lambda i: ring_copy(which, buffer, i).start())

    def ring_finish(which, buffer):
        def wait(i):
            other = lax.rem(z + i, zs)
            pltpu.make_async_remote_copy(
                src_ref=buffer.at[other],
                dst_ref=buffer.at[other],
                send_sem=s2.at[which, other],
                recv_sem=r2.at[which, other],
                device_id=(ring_device(other),),
                device_id_type=MESH,
            ).wait_recv()

        times(zs, wait)
        return jnp.sum(buffer[...], axis=0)

    def plane_sent(which, buffer):
        times(group, lambda i: plane_copy(which, buffer, i).wait_send())

    def ring_sent(which, buffer):
        times(zs, lambda i: ring_copy(which, buffer, i).wait_send())

    with jax.named_scope("diagonal"):
        load_d.wait()
        on_diagonal = iota((BS, BS), 0) == iota((BS, BS), 1)

        def add_diagonal(g, total):
            return total + jnp.where(on_diagonal, stage[g, 2], 0.0)

        total = lax.fori_loop(0, block_rows, add_diagonal, jnp.zeros((BS, BS), F32), unroll=4)
        mean = jnp.sum(total * (1.0 / (block_rows * BS)), axis=0, keepdims=True)

    with jax.named_scope("barrier_wait"):
        pl.semaphore_wait(barrier, 6 + group - 1 + zs - 1)
    with jax.named_scope("send0"):
        send_links(0)
        plane_start(0, sig1, mean)

    with jax.named_scope("split_band"):

        @pl.loop(0, pairs)
        def _(p):
            load_band(p, 0).wait()
            load_band(p, 1).wait()
            for local in range(2):
                for slot in range(5):
                    away = local + slot - 2
                    q = away // 2
                    hi, lo = split(stage[2 * p + local, slot])
                    top = (1 - q) * W + local * BS
                    lanes = pl.ds((away % 2) * BS, BS)
                    tiles[p + q + 1, pl.ds(top, BS), lanes] = hi
                    tiles[p + q + 1, pl.ds(3 * W + top, BS), lanes] = lo

    def band_product():
        def body(q):
            lhs = xs[:, pl.ds(pl.multiple_of(W * q, W), 3 * W)]
            out = dot(lhs, tiles[q + 1, pl.ds(0, 3 * W)]) + dot(lhs, tiles[q + 1, pl.ds(3 * W, 3 * W)])
            yb[q] = halves(out)

        each_pair(body)

    def landed(buffer, p):
        def of_row(g):
            total = buffer[0, inv[g * 6]]
            for j in range(1, 6):
                total = total + buffer[j, inv[g * 6 + j]]
            return total

        return yb[p] + jnp.concatenate([of_row(2 * p), of_row(2 * p + 1)], axis=1)

    def wait_halo(step):
        for j in range(6):
            halo_copy(step, j).wait_recv()

    with jax.named_scope("band0"):
        band_product()
    with jax.named_scope("halo0"):
        wait_halo(0)

    def store_w1(p):
        value = landed(recv0, p)
        w1[p] = value
        put(p, value, None)

    with jax.named_scope("land0"):
        each_pair(store_w1)

    with jax.named_scope("links1"):
        multiply_links(1)
        send_links(1)
    with jax.named_scope("sig_ring"):
        ring_start(0, sig2, plane_finish(0, sig1))
    with jax.named_scope("band1"):
        band_product()
    with jax.named_scope("halo1"):
        wait_halo(1)
    with jax.named_scope("sig_wait"):
        sigma = jnp.sum(ring_finish(0, sig2) * (1.0 / n), axis=1, keepdims=True)
        scale = 1.0 / sigma

    def store_v2(p):
        first = w1[p]
        one = first * scale - first_field(p)
        keep(p, 1, *split(one))
        two = (landed(recv1, p) * scale - first) * scale - one
        v2[p] = two
        put(p, two, 2)

    with jax.named_scope("land1"):
        each_pair(store_v2)

    with jax.named_scope("links2"):
        multiply_links(2)
        send_links(2)
    lane = iota((S, BS), 1)
    place = lax.div(lane, S) == lax.rem(iota((S, BS), 0), 8)
    with jax.named_scope("grams"):
        stack = jnp.concatenate([vs[pl.ds(0, 3 * S)], vs[pl.ds(4 * S, 3 * S)]], axis=0)
        grams = dot_nt(stack, stack)
        grams = grams[: 3 * S] + grams[3 * S :]
        grams = grams[:, : 3 * S] + grams[:, 3 * S :]

        def gram_of(a, b):
            return grams[S * a : S * a + S, S * b : S * b + S]

        pairs_of = ((0, 0), (0, 1), (1, 1), (1, 2), (2, 2))
        plane_start(1, gra1, jnp.stack([pack(gram_of(a, b), place) for a, b in pairs_of]))
    with jax.named_scope("band2"):
        band_product()

        def split_y(p):
            hi, lo = split(yb[p])
            ys[:, pl.ds(pl.multiple_of(W * p, W), W)] = jnp.concatenate([hi, lo], axis=0)

        each_pair(split_y)
    with jax.named_scope("gram_y"):
        field = jnp.concatenate([vs[pl.ds(2 * S, S)], vs[pl.ds(6 * S, S)]], axis=0)
        partial = halves(dot_nt(field, ys[pl.ds(0, S)]) + dot_nt(field, ys[pl.ds(S, S)]))
        partial = partial * scale - gram_of(2, 2)
        slots = [(j, s) for j in range(6) for s in range(H)]
        mine = jnp.concatenate([row_of(j, s) for j, s in slots], axis=1)
    with jax.named_scope("halo2"):
        wait_halo(2)
    with jax.named_scope("gram_c"):
        came = [split(recv2[j, s + 1]) for j, s in slots]
        arrived = dot_nt(mine, jnp.concatenate([hi for hi, _ in came], axis=1))
        arrived = arrived + dot_nt(mine, jnp.concatenate([lo for _, lo in came], axis=1))
        last = partial + halves(arrived) * scale
        plane_start(2, grb1, pack(last, place))

    def store_v3(p):
        keep(p, 3, *split(landed(recv2, p) * scale - v2[p]))

    with jax.named_scope("land2"):
        each_pair(store_v3)
    with jax.named_scope("gra_plane"):
        ring_start(1, gra2, plane_finish(1, gra1))
    with jax.named_scope("sent"):
        for step in range(3):
            for j in range(6):
                halo_copy(step, j).wait_send()
        plane_sent(0, sig1)
        ring_sent(0, sig2)
        plane_sent(1, gra1)
    with jax.named_scope("grb_plane"):
        ring_start(2, grb2, plane_finish(2, grb1))
    with jax.named_scope("gra_ring"):
        moments = ring_finish(1, gra2)

    with jax.named_scope("early"):
        m = [unpack(moments[k], place) for k in range(5)]

        def across(parts):
            total = jnp.where(lane < S, parts[0], 0.0)
            for k in (1, 2):
                total = jnp.where((lane >= S * k) & (lane < S * (k + 1)), parts[k], total)
            return total

        table = jnp.concatenate(
            [
                across([m[1] + m[0], m[2] + m[1], m[3] + m[2]]),
                across([m[2] + m[1], m[3] + m[2], m[4] + m[3]]),
                across([m[3] + m[2], m[4] + m[3], m[4]]),
                across([m[0], m[1], m[2]]),
            ],
            axis=0,
        )
        table = eliminate(table, 0, S)[S:]
        table = eliminate(table, S, S)[S:]
        middle, right = table[:S], table[S:]
        early = lane < 2 * S
        gain = jnp.where(early, middle, jnp.where(lane == 2 * S + iota((S, BS), 0), -1.0, 0.0))
        base = jnp.where(early, right, 0.0)

        def of_outputs(coeffs):
            both = jnp.concatenate([coeffs * scale, -(coeffs + pltpu.roll(coeffs, S, 1))], axis=0)
            return both + pltpu.roll(both, 4 * S, 1)

        gain, base = of_outputs(gain), of_outputs(base)
        upper = [jnp.broadcast_to(middle[:, 2 * S + j : 2 * S + j + 1], (S, BS)) for j in range(S)]
        lower = [jnp.broadcast_to(right[:, 2 * S + j : 2 * S + j + 1], (S, BS)) for j in range(S)]
        from_lane = lax.rem(iota((S, BS), 0), 8) * S
        plane_sent(2, grb1)
        ring_sent(1, gra2)

    with jax.named_scope("grb_ring"):
        late = ring_finish(2, grb2)
    with jax.named_scope("late"):
        late = widen(late)
        for j in range(S):
            upper[j] = upper[j] + jnp.sum(jnp.where(lane == from_lane + j, late, 0.0), axis=1, keepdims=True)
        columns = eliminate_columns(upper, lower)
        both = base
        for j in range(S):
            both = both - jnp.concatenate(
                [columns[j] * gain[j : j + 1], columns[j] * gain[S + j : S + j + 1]], axis=0
            )
        hi, lo = split(both)
        mixer = jnp.concatenate([hi, lo], axis=0)

    def mix(p):
        out = dot(mixer, vs[:, pl.ds(pl.multiple_of(W * p, W), W)])
        out = out[: 2 * S] + out[2 * S :]
        for local in range(2):
            lanes = slice(BS * local, BS * local + BS)
            x_out[2 * p + local] = out[:S, lanes]
            r_out[2 * p + local] = v0[2 * p + local] + out[S:, lanes]

    with jax.named_scope("mix"):
        each_pair(mix)
    with jax.named_scope("tail"):
        ring_sent(2, grb2)


def write_out(x, r, x_out, r_out, sem):
    copies = [pltpu.make_async_copy(x, x_out, sem.at[0]), pltpu.make_async_copy(r, r_out, sem.at[1])]
    for copy in copies:
        copy.start()
    for copy in copies:
        copy.wait()


def solution(mesh):
    n = mesh.devices.size
    zs = max(n // 32, 2)
    group = n // zs

    def local(right_side, band_blocks, link_blocks, link_rows):
        block_rows = right_side.shape[0]
        pairs = block_rows // 2
        field = jax.ShapeDtypeStruct(right_side.shape, F32)
        vmem = pltpu.VMEM
        dma = pltpu.SemaphoreType.DMA
        hbm = pl.BlockSpec(memory_space=pl.ANY)
        local_vmem = pl.BlockSpec(memory_space=pltpu.VMEM)
        outs = pl.pallas_call(
            functools.partial(kernel, n, zs),
            out_shape=(pltpu.VMEM(right_side.shape, F32),) * 2,
            in_specs=[pl.BlockSpec(memory_space=pltpu.HBM)] * 4,
            out_specs=(local_vmem,) * 2,
            scratch_shapes=[
                pltpu.SMEM((1, H, 6), jnp.int32),
                vmem((block_rows, S, BS), F32),
                vmem((block_rows, 5, BS, BS), F32),
                vmem((6, H, BS, BS), F32),
                vmem((pairs + 2, 6 * W, W), BF16),
                vmem((6, H, W, BS), BF16),
                vmem((8 * S, W * pairs), BF16),
                vmem((2 * S, W * (pairs + 2)), BF16),
                vmem((block_rows, 2 * S, BS), BF16),
                vmem((pairs, S, W), F32),
                vmem((2 * S, W * pairs), BF16),
                vmem((pairs, S, W), F32),
                vmem((pairs, S, W), F32),
                pltpu.SMEM((block_rows * 6,), jnp.int32),
                vmem((3, 6, H, S, BS), F32),
                vmem((6, H + 1, S, BS), F32),
                vmem((6, H + 1, S, BS), F32),
                vmem((6, H + 1, S, BS), F32),
                vmem((group, 1, BS), F32),
                vmem((zs, 1, BS), F32),
                vmem((group, 5, 2, BS), F32),
                vmem((zs, 5, 2, BS), F32),
                vmem((group, 2, BS), F32),
                vmem((zs, 2, BS), F32),
                dma((4,)),
                dma((pairs, 2)),
                dma((3, 6)),
                dma((3, 6)),
                dma((3, group)),
                dma((3, group)),
                dma((3, zs)),
                dma((3, zs)),
            ],
            compiler_params=pltpu.CompilerParams(
                collective_id=0, has_side_effects=True, vmem_limit_bytes=64904 * 1024
            ),
        )(
            *(
                pltpu.with_memory_space_constraint(x, pltpu.HBM)
                for x in (right_side, band_blocks, link_blocks, jnp.transpose(link_rows, (0, 2, 1)))
            )
        )
        return pl.pallas_call(
            write_out,
            out_shape=(field, field),
            in_specs=[local_vmem] * 2,
            out_specs=(hbm, hbm),
            scratch_shapes=[dma((2,))],
        )(*(pltpu.with_memory_space_constraint(o, pltpu.VMEM) for o in outs))

    return jax.shard_map(
        local,
        mesh=mesh,
        in_specs=(P("dom", None, None), P("dom", None, None, None), P("dom", None, None, None, None), P("dom", None, None)),
        out_specs=(P("dom", None, None), P("dom", None, None)),
        check_vma=False,
    )
```

time: 51.5 us -> 41 us (0.80)
  Pallas kernels: 46 us -> 40.3 us
  local copies, waits for them, and re-layouts: 4.69 us -> 0 us
    pallas_call x1 -> x2, Pallas kernels: 46 us -> 40.3 us  [the longest x1 39.5 us: local(): pl.pallas_call(functools.partial(kernel, n, zs), out_shape=(pltpu.VMEM(ri...]
    unnamed x3 -> x0, local copies, waits for them, and re-layouts: 4.69 us -> none
where the time goes in v2:
time: 41 us
  Pallas kernels  40.3 us (98%)
  between operations  0.64 us (2%)
    pallas_call x1, Pallas kernels, local(): pl.pallas_call(functools.partial(kernel, n, zs), out_shape=(pltpu.VMEM(ri...  39.5 us

profile of v2, /device:TPU:1, one launch (start us, length us, event | category | flops | bytes accessed | tf_op | source)
XLA Modules:
  0.0 41.0 jit_solution(981838482446767523)
XLA Ops:
  0.6 39.5 %shard_map.59 = (f32[32,16,128]{2,1,0:T(8,128)S(1)}, f32[32,16,128]{2,1,0:T(8,128)S(1)}) custom-call(f32[32,16,128]{2,1,0:T(8,128)} %rhs.1, f32[32,5,128,128]{3,2,1,0:T(8,128)} %band.1, f32[1,6,4,128,128]{4,3,2,1,0:T(8,128)} %link.1, s32[1,4,6]{2,1,0:T(4,128)} %bitcast.1), custom_call_target="tpu_custom_call" | custom-call | tf_op jit(solution)/shard_map/pallas_call | solution.py:567
  40.1 0.8 %shard_map.60 = (f32[32,16,128]{2,1,0:T(8,128)}, f32[32,16,128]{2,1,0:T(8,128)}) custom-call(f32[32,16,128]{2,1,0:T(8,128)S(1)} %get-tuple-element.4.x, f32[32,16,128]{2,1,0:T(8,128)S(1)} %get-tuple-element.5.r), custom_call_target="tpu_custom_call" | custom-call | tf_op jit(solution)/shard_map/pallas_call | solution.py:615

commit v3 on v2

v3 whole, which is shorter than its diff:
```python
import functools

import jax
import jax.numpy as jnp
from jax import lax
from jax.experimental import pallas as pl
from jax.experimental.pallas import tpu as pltpu
from jax.sharding import PartitionSpec as P

S = 16
BS = 128
W = 2 * BS
H = 4
MESH = pl.DeviceIdType.MESH
F32 = jnp.float32
BF16 = jnp.bfloat16


def dot(a, b):
    return jnp.dot(a, b, preferred_element_type=F32)


def dot_nt(a, b):
    return lax.dot_general(a, b, (((1,), (1,)), ((), ())), preferred_element_type=F32)


def split(x):
    hi = x.astype(BF16)
    return hi, (x - hi.astype(F32)).astype(BF16)


def halves(x):
    return x[:S] + x[S:]


def iota(shape, dim):
    return lax.broadcasted_iota(jnp.int32, shape, dim)


def eliminate(upper, lower):
    count = len(upper)
    for k in range(count):
        inverse = 1.0 / upper[k][k : k + 1]
        up, low = upper[k] * inverse, lower[k] * inverse
        for j in range(count):
            if j != k:
                factor = upper[j][k : k + 1]
                upper[j], lower[j] = upper[j] - up * factor, lower[j] - low * factor
        upper[k], lower[k] = up, low
    return lower


def sweep(table, first):
    lane = iota((S, BS), 1)
    rows = table.shape[0] - S

    def spread(part, k, height):
        return jnp.broadcast_to(part[:, first + k : first + k + 1], (height, BS))

    top, rest = table[:S], table[S:]
    columns = eliminate([spread(top, k, S) for k in range(S)], [spread(rest, k, rows) for k in range(S)])
    mine = (lane >= first) & (lane < first + S)
    top = jnp.where(lane == first + iota((S, BS), 0), -1.0, jnp.where(mine, 0.0, top))
    lane = iota((1, BS), 1)
    rest = jnp.where((lane >= first) & (lane < first + S), 0.0, rest)
    for k in range(S):
        rest = rest - columns[k] * top[k : k + 1]
    return rest


def pack(gram, place):
    spread = jnp.where(place, jnp.concatenate([gram] * 8, axis=1), 0.0)
    return jnp.concatenate(
        [jnp.sum(spread[:8], axis=0, keepdims=True), jnp.sum(spread[8:], axis=0, keepdims=True)], axis=0
    )


def widen(packed):
    return jnp.concatenate(
        [jnp.broadcast_to(packed[:1], (8, BS)), jnp.broadcast_to(packed[1:], (8, BS))], axis=0
    )


def unpack(packed, place):
    spread = jnp.where(place, widen(packed), 0.0)
    for shift in (64, 32, 16):
        spread = spread + pltpu.roll(spread, shift, 1)
    return spread


def kernel(
    n,
    zs,
    rhs,
    band,
    link,
    rows_in,
    v0,
    vs,
    mixer_out,
    rows,
    stage,
    lstage,
    tiles,
    links,
    xs,
    vr,
    yb,
    ys,
    w1,
    v2,
    inv,
    send,
    recv0,
    recv1,
    recv2,
    sig1,
    sig2,
    gra1,
    gra2,
    grb1,
    grb2,
    in_sem,
    band_sem,
    halo_send,
    halo_recv,
    s1,
    r1,
    s2,
    r2,
):
    block_rows = v0.shape[0]
    pairs = block_rows // 2
    group = n // zs
    me = lax.axis_index("dom")
    offsets = (1, n - 1, n // 16, n - n // 16, n // 4, n - n // 4)
    z = lax.rem(lax.div(me, 2), zs)
    rank = lax.div(me, 2 * zs) * 2 + lax.rem(me, 2)

    def hops(i):
        return sum((0, 1, 2, 1)[i >> at & 3] for at in (1, 3))

    plane_masks = [i // 2 * 2 * zs + i % 2 for i in sorted(range(1, group), key=hops, reverse=True)]
    ring_masks = [2 * i for i in sorted(range(1, zs), key=(0, 1, 3, 2, 7, 6, 5, 4).index if zs == 8 else None, reverse=True)]

    barrier = pltpu.get_barrier_semaphore()

    def announce(device):
        pl.semaphore_signal(barrier, inc=1, device_id=(device,), device_id_type=MESH)

    load_r = pltpu.make_async_copy(rows_in, rows, in_sem.at[0])
    load_v = pltpu.make_async_copy(rhs, v0, in_sem.at[1])
    load_l = pltpu.make_async_copy(link.at[0], lstage, in_sem.at[2])
    load_d = pltpu.make_async_copy(band.at[:, 2], stage.at[:, 2], in_sem.at[3])
    quarter = pairs // 4

    def load_band(c, side):
        at = (pl.ds(2 * quarter * c, 2 * quarter), pl.ds(3 * side, 2))
        return pltpu.make_async_copy(band.at[at], stage.at[at], band_sem.at[c, side])

    with jax.named_scope("signals"):
        for offset in offsets:
            announce(lax.rem(me + offset, n))
        load_r.start()
        load_v.start()
        load_l.start()
        load_d.start()
        for c in range(4):
            load_band(c, 0).start()
            load_band(c, 1).start()
        for mask in ring_masks + plane_masks:
            announce(me ^ mask)

    with jax.named_scope("zeros"):
        for buffer in (recv0, recv1, recv2):
            buffer[:, 0] = jnp.zeros((6, S, BS), F32)
        xs[:, pl.ds(0, W)] = jnp.zeros((2 * S, W), BF16)
        xs[:, pl.ds(W * (pairs + 1), W)] = jnp.zeros((2 * S, W), BF16)
        for part in range(2):
            tiles[1, pl.ds(part * 3 * W, W)] = jnp.zeros((W, W), BF16)
            tiles[pairs, pl.ds(part * 3 * W + 2 * W, W)] = jnp.zeros((W, W), BF16)

    def each_pair(body):
        def step(p, carry):
            body(p)
            return carry

        lax.fori_loop(0, pairs, step, 0, unroll=True)

    def put(p, value, slot):
        hi, lo = split(value)
        both = jnp.concatenate([hi, lo], axis=0)
        xs[:, pl.ds(pl.multiple_of(W * (p + 1), W), W)] = both
        vr[2 * p] = both[:, :BS]
        vr[2 * p + 1] = both[:, BS:]
        if slot is not None:
            keep(p, slot, hi, lo)

    def keep(p, slot, hi, lo):
        lanes = pl.ds(pl.multiple_of(W * p, W), W)
        vs[pl.ds(S * slot, S), lanes] = hi
        vs[pl.ds(4 * S + S * slot, S), lanes] = lo

    def first_field(p):
        return jnp.concatenate([v0[2 * p], v0[2 * p + 1]], axis=1)

    with jax.named_scope("load_v"):
        load_v.wait()
        each_pair(lambda p: put(p, first_field(p), 0))

    with jax.named_scope("load_l"):
        load_l.wait()
        for j in range(6):
            for s in range(H):
                hi, lo = split(lstage[j, s])
                links[j, s, pl.ds(0, BS)] = hi
                links[j, s, pl.ds(BS, BS)] = lo

    def halo_copy(step, j):
        return pltpu.make_async_remote_copy(
            src_ref=send.at[step, j],
            dst_ref=(recv0, recv1, recv2)[step].at[j ^ 1, pl.ds(1, H)],
            send_sem=halo_send.at[step],
            recv_sem=halo_recv.at[step],
            device_id=(lax.rem(me + offsets[j], n),),
            device_id_type=MESH,
        )

    def own_row(j, s):
        return jnp.minimum(rows[0, s, j], block_rows - 1)

    def multiply_link(step, j, s, mine):
        send[step, j, s] = halves(dot(jnp.concatenate([mine, mine], axis=1), links[j, s]))

    def multiply_links(step, interfaces):
        for j in interfaces:
            for s in range(H):
                multiply_link(step, j, s, vr[own_row(j, s)])

    def start_links(step, interfaces):
        for j in interfaces:
            halo_copy(step, j).start()

    def send_links(step, store):
        for j in (0, 1):
            for s in range(H):
                hi, lo = split(row_value(step - 1, own_row(j, s)))
                multiply_link(step, j, s, jnp.concatenate([hi, lo], axis=0))
        start_links(step, (0, 1))
        each_pair(store)
        multiply_links(step, (2, 3, 4, 5))
        start_links(step, (2, 3, 4, 5))

    def all_links(step):
        return pltpu.make_async_remote_copy(
            src_ref=send.at[step],
            dst_ref=(recv0, recv1, recv2)[step].at[:, pl.ds(1, H)],
            send_sem=halo_send.at[step],
            recv_sem=halo_recv.at[step],
            device_id=(lax.rem(me + 1, n),),
            device_id_type=MESH,
        )

    with jax.named_scope("links0"):
        load_r.wait()
        multiply_links(0, range(6))

    def plane_start(which, buffer, value):
        buffer[rank] = value
        for mask in plane_masks:
            pltpu.make_async_remote_copy(
                src_ref=buffer.at[rank],
                dst_ref=buffer.at[rank],
                send_sem=s1.at[which],
                recv_sem=r1.at[which],
                device_id=(me ^ mask,),
                device_id_type=MESH,
            ).start()

    def all_plane(which, buffer):
        others = buffer.at[pl.ds(0, group - 1)]
        return pltpu.make_async_remote_copy(
            src_ref=others,
            dst_ref=others,
            send_sem=s1.at[which],
            recv_sem=r1.at[which],
            device_id=(me ^ plane_masks[0],),
            device_id_type=MESH,
        )

    def plane_finish(which, buffer):
        all_plane(which, buffer).wait_recv()
        return jnp.sum(buffer[...], axis=0)

    def ring_start(which, buffer, value):
        buffer[z] = value
        for mask in ring_masks:
            pltpu.make_async_remote_copy(
                src_ref=buffer.at[z],
                dst_ref=buffer.at[z],
                send_sem=s2.at[which],
                recv_sem=r2.at[which],
                device_id=(me ^ mask,),
                device_id_type=MESH,
            ).start()

    def all_ring(which, buffer):
        others = buffer.at[pl.ds(0, zs - 1)]
        return pltpu.make_async_remote_copy(
            src_ref=others,
            dst_ref=others,
            send_sem=s2.at[which],
            recv_sem=r2.at[which],
            device_id=(me ^ ring_masks[0],),
            device_id_type=MESH,
        )

    def ring_finish(which, buffer):
        all_ring(which, buffer).wait_recv()
        return jnp.sum(buffer[...], axis=0)

    def plane_sent(which, buffer):
        all_plane(which, buffer).wait_send()

    def ring_sent(which, buffer):
        all_ring(which, buffer).wait_send()

    at = [[rows[0, s, j] for s in range(H)] for j in range(6)]
    zero_block = jnp.zeros((BS, BS), BF16)

    def split_band(c):
        load_band(c, 0).wait()
        load_band(c, 1).wait()

        @pl.loop(quarter * c, quarter * (c + 1))
        def _(p):
            for local in range(2):
                g = 2 * p + local
                for slot in range(5):
                    away = local + slot - 2
                    q = away // 2
                    hi, lo = split(stage[g, slot])
                    top = (1 - q) * W + local * BS
                    lanes = pl.ds((away % 2) * BS, BS)
                    tiles[p + q + 1, pl.ds(top, BS), lanes] = hi
                    tiles[p + q + 1, pl.ds(3 * W + top, BS), lanes] = lo
                for j in range(6):
                    found = 0
                    for s in range(H):
                        found = jnp.where(at[j][s] == g, s + 1, found)
                    inv[g * 6 + j] = found
            for part in range(2):
                tiles[p + 1, pl.ds(part * 3 * W, BS), pl.ds(BS, BS)] = zero_block
                tiles[p + 1, pl.ds(part * 3 * W + 2 * W + BS, BS), pl.ds(0, BS)] = zero_block

    def split_all():
        for c in range(4):
            split_band(c)

    steps = lax.div(me, 2 * zs)
    early = lax.rem(steps, 4) + lax.div(steps, 4) + z < 6

    @pl.when(early)
    def _():
        load_d.wait()
        split_all()

    with jax.named_scope("barrier_wait"):
        pl.semaphore_wait(barrier, 6 + group - 1 + zs - 1)
    with jax.named_scope("send0"):
        start_links(0, range(6))
    @pl.when(jnp.logical_not(early))
    def _():
        load_d.wait()

    with jax.named_scope("diagonal"):
        on_diagonal = iota((BS, BS), 0) == iota((BS, BS), 1)

        def add_diagonal(g, total):
            return total + jnp.where(on_diagonal, stage[g, 2], 0.0)

        total = lax.fori_loop(0, block_rows, add_diagonal, jnp.zeros((BS, BS), F32), unroll=4)
        mean = jnp.sum(total * (1.0 / (block_rows * BS)), axis=0, keepdims=True)
        plane_start(0, sig1, mean)

    @pl.when(jnp.logical_not(early))
    def _():
        split_all()

    def band_product():
        def body(q):
            lhs = xs[:, pl.ds(pl.multiple_of(W * q, W), 3 * W)]
            out = dot(lhs, tiles[q + 1, pl.ds(0, 3 * W)]) + dot(lhs, tiles[q + 1, pl.ds(3 * W, 3 * W)])
            out = halves(out)
            yb[2 * q], yb[2 * q + 1] = out[:, :BS], out[:, BS:]

        each_pair(body)

    def row_value(step, g):
        total = yb[g]
        for j in range(6):
            total = total + (recv0, recv1, recv2)[step][j, inv[g * 6 + j]]
        if step == 0:
            return total
        if step == 1:
            return (total * scale - w1[g]) * scale - (w1[g] * scale - v0[g])
        return total * scale - v2[g]

    def pair_value(step, p):
        return jnp.concatenate([row_value(step, 2 * p), row_value(step, 2 * p + 1)], axis=1)

    def wait_halo(step):
        all_links(step).wait_recv()

    with jax.named_scope("band0"):
        band_product()
    with jax.named_scope("halo0"):
        wait_halo(0)

    def store_w1(p):
        value = pair_value(0, p)
        w1[2 * p], w1[2 * p + 1] = value[:, :BS], value[:, BS:]
        put(p, value, None)


    with jax.named_scope("links1"):
        send_links(1, store_w1)
    with jax.named_scope("sig_ring"):
        ring_start(0, sig2, plane_finish(0, sig1))
    with jax.named_scope("band1"):
        band_product()
    with jax.named_scope("halo1"):
        wait_halo(1)
    with jax.named_scope("sig_wait"):
        sigma = jnp.sum(ring_finish(0, sig2) * (1.0 / n), axis=1, keepdims=True)
        scale = 1.0 / sigma

    def store_v2(p):
        first = jnp.concatenate([w1[2 * p], w1[2 * p + 1]], axis=1)
        keep(p, 1, *split(first * scale - first_field(p)))
        value = pair_value(1, p)
        v2[2 * p], v2[2 * p + 1] = value[:, :BS], value[:, BS:]
        put(p, value, 2)

    with jax.named_scope("links2"):
        send_links(2, store_v2)
    lane = iota((S, BS), 1)
    place = lax.div(lane, S) == lax.rem(iota((S, BS), 0), 8)
    with jax.named_scope("grams"):
        stack = jnp.concatenate([vs[pl.ds(0, 3 * S)], vs[pl.ds(4 * S, 3 * S)]], axis=0)
        grams = dot_nt(stack, stack)
        grams = grams[: 3 * S] + grams[3 * S :]
        grams = grams[:, : 3 * S] + grams[:, 3 * S :]

        def gram_of(a, b):
            return grams[S * a : S * a + S, S * b : S * b + S]

        pairs_of = ((0, 0), (0, 1), (1, 1), (1, 2), (2, 2))
        plane_start(1, gra1, jnp.stack([pack(gram_of(a, b), place) for a, b in pairs_of]))
    with jax.named_scope("band2"):
        band_product()

        def split_y(p):
            hi, lo = split(jnp.concatenate([yb[2 * p], yb[2 * p + 1]], axis=1))
            ys[:, pl.ds(pl.multiple_of(W * p, W), W)] = jnp.concatenate([hi, lo], axis=0)

        each_pair(split_y)
    with jax.named_scope("gram_y"):
        field = jnp.concatenate([vs[pl.ds(2 * S, S)], vs[pl.ds(6 * S, S)]], axis=0)
        partial = halves(dot_nt(field, ys[pl.ds(0, S)]) + dot_nt(field, ys[pl.ds(S, S)]))
        partial = partial * scale - gram_of(2, 2)
        slots = [(j, s) for j in range(6) for s in range(H)]
        mine = jnp.concatenate([vr[own_row(j, s)] for j, s in slots], axis=1)
    with jax.named_scope("halo2"):
        wait_halo(2)
    with jax.named_scope("gram_c"):
        came = [split(recv2[j, s + 1]) for j, s in slots]
        arrived = dot_nt(mine, jnp.concatenate([hi for hi, _ in came], axis=1))
        arrived = arrived + dot_nt(mine, jnp.concatenate([lo for _, lo in came], axis=1))
        last = partial + halves(arrived) * scale
        plane_start(2, grb1, pack(last, place))

    def store_v3(p):
        keep(p, 3, *split(pair_value(2, p)))

    with jax.named_scope("land2"):
        each_pair(store_v3)
    with jax.named_scope("gra_plane"):
        ring_start(1, gra2, plane_finish(1, gra1))
    with jax.named_scope("sent"):
        for step in range(3):
            all_links(step).wait_send()
        plane_sent(0, sig1)
        ring_sent(0, sig2)
        plane_sent(1, gra1)
    with jax.named_scope("grb_plane"):
        ring_start(2, grb2, plane_finish(2, grb1))
    with jax.named_scope("gra_ring"):
        moments = ring_finish(1, gra2)

    with jax.named_scope("early"):
        m = [unpack(moments[k], place) for k in range(5)]

        def across(parts):
            total = jnp.where(lane < S, parts[0], 0.0)
            for k in (1, 2):
                total = jnp.where((lane >= S * k) & (lane < S * (k + 1)), parts[k], total)
            return total

        table = jnp.concatenate(
            [
                across([m[1] + m[0], m[2] + m[1], m[3] + m[2]]),
                across([m[2] + m[1], m[3] + m[2], m[4] + m[3]]),
                across([m[3] + m[2], m[4] + m[3], m[4]]),
                across([m[0], m[1], m[2]]),
            ],
            axis=0,
        )
        table = sweep(sweep(table, 0), S)
        middle, right = table[:S], table[S:]
        known = lane < 2 * S
        gain = jnp.where(known, middle, jnp.where(lane == 2 * S + iota((S, BS), 0), -1.0, 0.0))
        base = jnp.where(known, right, 0.0)

        def of_outputs(coeffs):
            both = jnp.concatenate([coeffs * scale, -(coeffs + pltpu.roll(coeffs, S, 1))], axis=0)
            return both + pltpu.roll(both, 4 * S, 1)

        gain, base = of_outputs(gain), of_outputs(base)
        upper = [jnp.broadcast_to(middle[:, 2 * S + j : 2 * S + j + 1], (S, BS)) for j in range(S)]
        lower = [jnp.broadcast_to(right[:, 2 * S + j : 2 * S + j + 1], (S, BS)) for j in range(S)]
        from_lane = lax.rem(iota((S, BS), 0), 8) * S
        plane_sent(2, grb1)
        ring_sent(1, gra2)

    with jax.named_scope("grb_ring"):
        late = ring_finish(2, grb2)
    with jax.named_scope("late"):
        late = widen(late)
        for j in range(S):
            upper[j] = upper[j] + jnp.sum(jnp.where(lane == from_lane + j, late, 0.0), axis=1, keepdims=True)
        columns = eliminate(upper, lower)
        both = base
        for j in range(S):
            both = both - jnp.concatenate(
                [columns[j] * gain[j : j + 1], columns[j] * gain[S + j : S + j + 1]], axis=0
            )
        hi, lo = split(both)
        mixer_out[...] = jnp.concatenate([hi, lo], axis=0)
        ring_sent(2, grb2)


def mix(v0, vs, mixer, x_out, r_out, x, r, sem):
    pairs = v0.shape[0] // 2
    half = v0.shape[0] // 2
    copies = []
    for part in range(2):
        for p in range(part * pairs // 2, (part + 1) * pairs // 2):
            out = dot(mixer[...], vs[:, pl.ds(W * p, W)])
            out = out[: 2 * S] + out[2 * S :]
            for local in range(2):
                lanes = slice(BS * local, BS * local + BS)
                x[2 * p + local] = out[:S, lanes]
                r[2 * p + local] = v0[2 * p + local] + out[S:, lanes]
        at = pl.ds(half * part, half)
        copies.append(pltpu.make_async_copy(x.at[at], x_out.at[at], sem.at[part, 0]))
        copies.append(pltpu.make_async_copy(r.at[at], r_out.at[at], sem.at[part, 1]))
        copies[-2].start()
        copies[-1].start()
    for copy in copies:
        copy.wait()


def solution(mesh):
    n = mesh.devices.size
    zs = max(n // 32, 2)
    group = n // zs

    def local(right_side, band_blocks, link_blocks, link_rows):
        block_rows = right_side.shape[0]
        pairs = block_rows // 2
        field = jax.ShapeDtypeStruct(right_side.shape, F32)
        vmem = pltpu.VMEM
        dma = pltpu.SemaphoreType.DMA
        hbm = pl.BlockSpec(memory_space=pl.ANY)
        local_vmem = pl.BlockSpec(memory_space=pltpu.VMEM)
        outs = pl.pallas_call(
            functools.partial(kernel, n, zs),
            out_shape=(vmem(field.shape, F32), vmem((8 * S, W * pairs), BF16), vmem((4 * S, BS), BF16)),
            in_specs=[pl.BlockSpec(memory_space=pltpu.HBM)] * 4,
            out_specs=(local_vmem,) * 3,
            scratch_shapes=[
                pltpu.SMEM((1, H, 6), jnp.int32),
                vmem((block_rows, 5, BS, BS), F32),
                vmem((6, H, BS, BS), F32),
                vmem((pairs + 2, 6 * W, W), BF16),
                vmem((6, H, W, BS), BF16),
                vmem((2 * S, W * (pairs + 2)), BF16),
                vmem((block_rows, 2 * S, BS), BF16),
                vmem(field.shape, F32),
                vmem((2 * S, W * pairs), BF16),
                vmem(field.shape, F32),
                vmem(field.shape, F32),
                pltpu.SMEM((block_rows * 6,), jnp.int32),
                vmem((3, 6, H, S, BS), F32),
                vmem((6, H + 1, S, BS), F32),
                vmem((6, H + 1, S, BS), F32),
                vmem((6, H + 1, S, BS), F32),
                vmem((group, 1, BS), F32),
                vmem((zs, 1, BS), F32),
                vmem((group, 5, 2, BS), F32),
                vmem((zs, 5, 2, BS), F32),
                vmem((group, 2, BS), F32),
                vmem((zs, 2, BS), F32),
                dma((4,)),
                dma((4, 2)),
                dma((3,)),
                dma((3,)),
                dma((3,)),
                dma((3,)),
                dma((3,)),
                dma((3,)),
            ],
            compiler_params=pltpu.CompilerParams(
                collective_id=0, has_side_effects=True, vmem_limit_bytes=62 * 1024 * 1024
            ),
        )(
            *(
                pltpu.with_memory_space_constraint(x, pltpu.HBM)
                for x in (right_side, band_blocks, link_blocks, jnp.transpose(link_rows, (0, 2, 1)))
            )
        )
        return pl.pallas_call(
            mix,
            out_shape=(field, field),
            in_specs=[local_vmem] * 3,
            out_specs=(hbm, hbm),
            scratch_shapes=[vmem(field.shape, F32), vmem(field.shape, F32), dma((2, 2))],
        )(*(pltpu.with_memory_space_constraint(o, pltpu.VMEM) for o in outs))

    return jax.shard_map(
        local,
        mesh=mesh,
        in_specs=(P("dom", None, None), P("dom", None, None, None), P("dom", None, None, None, None), P("dom", None, None)),
        out_specs=(P("dom", None, None), P("dom", None, None)),
        check_vma=False,
    )
```

time: 41 us -> 37.3 us (0.910)
  Pallas kernels: 40.3 us -> 36.6 us
    pallas_call x2, Pallas kernels: 40.3 us -> 36.6 us  [the longest x1 35.6 us: local(): pl.pallas_call(functools.partial(kernel, n, zs), out_shape=(vmem(field.sh...]
where the time goes in v3:
time: 37.3 us; the launch traced here: 37.2 us
  Pallas kernels  36.6 us (98%)
  between operations  0.64 us (2%)
    pallas_call x1, Pallas kernels, local(): pl.pallas_call(functools.partial(kernel, n, zs), out_shape=(vmem(field.sh...  35.6 us
    pallas_call x1, Pallas kernels, local(): pl.pallas_call(mix, out_shape=(field, field), in_specs=[local_vmem] * 3,...  1.04 us

profile of v3, /device:TPU:1, one launch (start us, length us, event | category | flops | bytes accessed | tf_op | source)
XLA Modules:
  0.0 37.2 jit_solution(11315431056296154439)
XLA Ops:
  0.6 35.6 %shard_map.59 = (f32[32,16,128]{2,1,0:T(8,128)S(1)}, bf16[128,4096]{1,0:T(8,128)(2,1)S(1)}, bf16[64,128]{1,0:T(8,128)(2,1)S(1)}) custom-call(f32[32,16,128]{2,1,0:T(8,128)} %rhs.1, f32[32,5,128,128]{3,2,1,0:T(8,128)} %band.1, f32[1,6,4,128,128]{4,3,2,1,0:T(8,128)} %link.1, s32[1,4,6]{2,1,0:T(4,128)} %bitcast.1), custom_call_target="tpu_custom_call" | custom-call | tf_op jit(solution)/shard_map/pallas_call | solution.py:587
  36.2 1.0 %shard_map.60 = (f32[32,16,128]{2,1,0:T(8,128)}, f32[32,16,128]{2,1,0:T(8,128)}) custom-call(f32[32,16,128]{2,1,0:T(8,128)S(1)} %get-tuple-element.5.v0, bf16[128,4096]{1,0:T(8,128)(2,1)S(1)} %get-tuple-element.6.vs, bf16[64,128]{1,0:T(8,128)(2,1)S(1)} %get-tuple-element.7.mixer), custom_call_target="tpu_custom_call" | custom-call | tf_op jit(solution)/shard_map/pallas_call | solution.py:633

commit v4 on v3

--- a/solution.py
+++ b/solution.py
@@ -114,6 +114,12 @@
     recv0,
     recv1,
     recv2,
+    far0,
+    far1,
+    far2,
+    farc,
+    mirror1,
+    mirror2,
     sig1,
     sig2,
     gra1,
@@ -133,7 +139,17 @@
     pairs = block_rows // 2
     group = n // zs
     me = lax.axis_index("dom")
-    offsets = (1, n - 1, n // 16, n - n // 16, n // 4, n - n // 4)
+    core = lax.rem(me, 2)
+    given = (1 - core, core, 2, 3, 4, 5)
+    facing = (
+        lax.rem(me + (n - 1) + 2 * core, n),
+        me ^ 1,
+        lax.rem(me + n // 16, n),
+        lax.rem(me + (n - n // 16), n),
+        lax.rem(me + n // 4, n),
+        lax.rem(me + (n - n // 4), n),
+    )
+    arrives_at = (0, 1, 3, 2, 5, 4)
     z = lax.rem(lax.div(me, 2), zs)
     rank = lax.div(me, 2 * zs) * 2 + lax.rem(me, 2)
 
@@ -159,8 +175,8 @@
         return pltpu.make_async_copy(band.at[at], stage.at[at], band_sem.at[c, side])
 
     with jax.named_scope("signals"):
-        for offset in offsets:
-            announce(lax.rem(me + offset, n))
+        for device in facing:
+            announce(device)
         load_r.start()
         load_v.start()
         load_l.start()
@@ -173,7 +189,9 @@
 
     with jax.named_scope("zeros"):
         for buffer in (recv0, recv1, recv2):
-            buffer[:, 0] = jnp.zeros((6, S, BS), F32)
+            buffer[:, 0] = jnp.zeros((5, S, BS), F32)
+        for buffer in (far0, farc):
+            buffer[0] = jnp.zeros((S, BS), F32)
         xs[:, pl.ds(0, W)] = jnp.zeros((2 * S, W), BF16)
         xs[:, pl.ds(W * (pairs + 1), W)] = jnp.zeros((2 * S, W), BF16)
         for part in range(2):
@@ -212,54 +230,80 @@
         load_l.wait()
         for j in range(6):
             for s in range(H):
-                hi, lo = split(lstage[j, s])
+                hi, lo = split(lstage[given[j], s])
                 links[j, s, pl.ds(0, BS)] = hi
                 links[j, s, pl.ds(BS, BS)] = lo
+
+    others = pl.ds(1, 5)
+    slots = pl.ds(1, H)
+    recvs, fars = (recv0, recv1, recv2), (far0, far1, far2)
 
     def halo_copy(step, j):
         return pltpu.make_async_remote_copy(
             src_ref=send.at[step, j],
-            dst_ref=(recv0, recv1, recv2)[step].at[j ^ 1, pl.ds(1, H)],
+            dst_ref=recvs[step].at[arrives_at[j] - 1, slots] if j else fars[step].at[slots],
             send_sem=halo_send.at[step],
-            recv_sem=halo_recv.at[step],
-            device_id=(lax.rem(me + offsets[j], n),),
+            recv_sem=halo_recv.at[step, min(j, 1)],
+            device_id=(facing[j],),
             device_id_type=MESH,
         )
 
     def own_row(j, s):
-        return jnp.minimum(rows[0, s, j], block_rows - 1)
-
-    def multiply_link(step, j, s, mine):
-        send[step, j, s] = halves(dot(jnp.concatenate([mine, mine], axis=1), links[j, s]))
+        return jnp.minimum(rows[0, s, given[j]], block_rows - 1)
+
+    def times_block(j, s, mine):
+        return halves(dot(jnp.concatenate([mine, mine], axis=1), links[j, s]))
+
+    def times_transpose(s, value):
+        both = jnp.concatenate(split(value), axis=0)
+        return halves(dot_nt(both, links[0, s, pl.ds(0, BS)]) + dot_nt(both, links[0, s, pl.ds(BS, BS)]))
 
     def multiply_links(step, interfaces):
         for j in interfaces:
             for s in range(H):
-                multiply_link(step, j, s, vr[own_row(j, s)])
+                send[step, j, s] = times_block(j, s, vr[own_row(j, s)])
 
     def start_links(step, interfaces):
         for j in interfaces:
             halo_copy(step, j).start()
 
     def send_links(step, store):
-        for j in (0, 1):
+        for s in range(H):
+            parts = split(row_value(step - 1, own_row(0, s), False))
+            send[step, 0, s] = times_block(0, s, jnp.concatenate(parts, axis=0))
+        start_links(step, (0,))
+        wait_far(step - 1)
+        each_pair(store)
+        for interfaces in ((2, 3), (4, 5, 1)):
+            multiply_links(step, interfaces)
+            start_links(step, interfaces)
+
+    def wait_far(step):
+        halo_copy(step, 0).wait_recv()
+        if step > 0:
             for s in range(H):
-                hi, lo = split(row_value(step - 1, own_row(j, s)))
-                multiply_link(step, j, s, jnp.concatenate([hi, lo], axis=0))
-        start_links(step, (0, 1))
-        each_pair(store)
-        multiply_links(step, (2, 3, 4, 5))
-        start_links(step, (2, 3, 4, 5))
-
-    def all_links(step):
-        return pltpu.make_async_remote_copy(
+                missing = mirror1[s] if step == 1 else mirror2[s] * (scale * scale)
+                farc[s + 1] = fars[step][s + 1] + missing
+
+    def wait_others(step):
+        pltpu.make_async_remote_copy(
+            src_ref=send.at[step, others],
+            dst_ref=recvs[step].at[:, slots],
+            send_sem=halo_send.at[step],
+            recv_sem=halo_recv.at[step, 1],
+            device_id=(facing[1],),
+            device_id_type=MESH,
+        ).wait_recv()
+
+    def links_sent(step):
+        pltpu.make_async_remote_copy(
             src_ref=send.at[step],
-            dst_ref=(recv0, recv1, recv2)[step].at[:, pl.ds(1, H)],
+            dst_ref=send.at[step],
             send_sem=halo_send.at[step],
-            recv_sem=halo_recv.at[step],
-            device_id=(lax.rem(me + 1, n),),
+            recv_sem=halo_recv.at[step, 1],
+            device_id=(facing[1],),
             device_id_type=MESH,
-        )
+        ).wait_send()
 
     with jax.named_scope("links0"):
         load_r.wait()
@@ -325,10 +369,10 @@
     def ring_sent(which, buffer):
         all_ring(which, buffer).wait_send()
 
-    at = [[rows[0, s, j] for s in range(H)] for j in range(6)]
+    at = [[rows[0, s, given[j]] for s in range(H)] for j in range(6)]
     zero_block = jnp.zeros((BS, BS), BF16)
 
-    def split_band(c):
+    def split_chunk(c, carry):
         load_band(c, 0).wait()
         load_band(c, 1).wait()
 
@@ -353,23 +397,25 @@
                 tiles[p + 1, pl.ds(part * 3 * W, BS), pl.ds(BS, BS)] = zero_block
                 tiles[p + 1, pl.ds(part * 3 * W + 2 * W + BS, BS), pl.ds(0, BS)] = zero_block
 
-    def split_all():
-        for c in range(4):
-            split_band(c)
+        return carry
 
     steps = lax.div(me, 2 * zs)
-    early = lax.rem(steps, 4) + lax.div(steps, 4) + z < 6
-
-    @pl.when(early)
+    away = jnp.minimum(lax.rem(steps, 4), 2) + jnp.minimum(lax.div(steps, 4), 2)
+    ahead = jnp.where(away == 2, 1, 0)
+    ahead = jnp.where(z == 3, 2, ahead)
+    ahead = jnp.where((z < 3) | (away < 2), 4, ahead)
+
+    @pl.when(ahead > 0)
     def _():
         load_d.wait()
-        split_all()
+
+    lax.fori_loop(0, ahead, split_chunk, 0)
 
     with jax.named_scope("barrier_wait"):
         pl.semaphore_wait(barrier, 6 + group - 1 + zs - 1)
     with jax.named_scope("send0"):
         start_links(0, range(6))
-    @pl.when(jnp.logical_not(early))
+    @pl.when(ahead == 0)
     def _():
         load_d.wait()
 
@@ -383,9 +429,7 @@
         mean = jnp.sum(total * (1.0 / (block_rows * BS)), axis=0, keepdims=True)
         plane_start(0, sig1, mean)
 
-    @pl.when(jnp.logical_not(early))
-    def _():
-        split_all()
+    lax.fori_loop(ahead, 4, split_chunk, 0)
 
     def band_product():
         def body(q):
@@ -396,10 +440,12 @@
 
         each_pair(body)
 
-    def row_value(step, g):
+    def row_value(step, g, with_far=True):
         total = yb[g]
-        for j in range(6):
-            total = total + (recv0, recv1, recv2)[step][j, inv[g * 6 + j]]
+        for j in range(1, 6):
+            total = total + recvs[step][j - 1, inv[g * 6 + j]]
+        if with_far:
+            total = total + (farc if step else far0)[inv[g * 6]]
         if step == 0:
             return total
         if step == 1:
@@ -409,13 +455,10 @@
     def pair_value(step, p):
         return jnp.concatenate([row_value(step, 2 * p), row_value(step, 2 * p + 1)], axis=1)
 
-    def wait_halo(step):
-        all_links(step).wait_recv()
-
     with jax.named_scope("band0"):
         band_product()
     with jax.named_scope("halo0"):
-        wait_halo(0)
+        wait_others(0)
 
     def store_w1(p):
         value = pair_value(0, p)
@@ -427,10 +470,14 @@
         send_links(1, store_w1)
     with jax.named_scope("sig_ring"):
         ring_start(0, sig2, plane_finish(0, sig1))
+    with jax.named_scope("mirror"):
+        for s in range(H):
+            mirror1[s] = times_transpose(s, send[0, 0, s])
+            mirror2[s] = times_transpose(s, times_block(0, s, vr[own_row(0, s)]))
     with jax.named_scope("band1"):
         band_product()
     with jax.named_scope("halo1"):
-        wait_halo(1)
+        wait_others(1)
     with jax.named_scope("sig_wait"):
         sigma = jnp.sum(ring_finish(0, sig2) * (1.0 / n), axis=1, keepdims=True)
         scale = 1.0 / sigma
@@ -469,15 +516,26 @@
         field = jnp.concatenate([vs[pl.ds(2 * S, S)], vs[pl.ds(6 * S, S)]], axis=0)
         partial = halves(dot_nt(field, ys[pl.ds(0, S)]) + dot_nt(field, ys[pl.ds(S, S)]))
         partial = partial * scale - gram_of(2, 2)
-        slots = [(j, s) for j in range(6) for s in range(H)]
-        mine = jnp.concatenate([vr[own_row(j, s)] for j, s in slots], axis=1)
+        mine = [
+            jnp.concatenate([vr[own_row(j, s)] for s in range(H)], axis=1) for j in range(6)
+        ]
+
+    def gram_of_arrived(own, came):
+        parts = [split(value) for value in came]
+        return dot_nt(own, jnp.concatenate([hi for hi, _ in parts], axis=1)) + dot_nt(
+            own, jnp.concatenate([lo for _, lo in parts], axis=1)
+        )
+
     with jax.named_scope("halo2"):
-        wait_halo(2)
+        wait_others(2)
+    with jax.named_scope("gram_o"):
+        came = [recv2[j, s + 1] for j in range(5) for s in range(H)]
+        partial = partial + halves(gram_of_arrived(jnp.concatenate(mine[1:], axis=1), came)) * scale
+    with jax.named_scope("far2"):
+        wait_far(2)
     with jax.named_scope("gram_c"):
-        came = [split(recv2[j, s + 1]) for j, s in slots]
-        arrived = dot_nt(mine, jnp.concatenate([hi for hi, _ in came], axis=1))
-        arrived = arrived + dot_nt(mine, jnp.concatenate([lo for _, lo in came], axis=1))
-        last = partial + halves(arrived) * scale
+        came = [farc[s + 1] for s in range(H)]
+        last = partial + halves(gram_of_arrived(mine[0], came)) * scale
         plane_start(2, grb1, pack(last, place))
 
     def store_v3(p):
@@ -489,7 +547,7 @@
         ring_start(1, gra2, plane_finish(1, gra1))
     with jax.named_scope("sent"):
         for step in range(3):
-            all_links(step).wait_send()
+            links_sent(step)
         plane_sent(0, sig1)
         ring_sent(0, sig2)
         plane_sent(1, gra1)
@@ -603,9 +661,15 @@
                 vmem(field.shape, F32),
                 pltpu.SMEM((block_rows * 6,), jnp.int32),
                 vmem((3, 6, H, S, BS), F32),
-                vmem((6, H + 1, S, BS), F32),
-                vmem((6, H + 1, S, BS), F32),
-                vmem((6, H + 1, S, BS), F32),
+                vmem((5, H + 1, S, BS), F32),
+                vmem((5, H + 1, S, BS), F32),
+                vmem((5, H + 1, S, BS), F32),
+                vmem((H + 1, S, BS), F32),
+                vmem((H + 1, S, BS), F32),
+                vmem((H + 1, S, BS), F32),
+                vmem((H + 1, S, BS), F32),
+                vmem((H, S, BS), F32),
+                vmem((H, S, BS), F32),
                 vmem((group, 1, BS), F32),
                 vmem((zs, 1, BS), F32),
                 vmem((group, 5, 2, BS), F32),
@@ -615,7 +679,7 @@
                 dma((4,)),
                 dma((4, 2)),
                 dma((3,)),
-                dma((3,)),
+                dma((3, 2)),
                 dma((3,)),
                 dma((3,)),
                 dma((3,)),

time: 37.3 us -> 37.4 us (level)
  no operation moved by 1% of the time
where the time goes in v4:
time: 37.4 us; the launch traced here: 37.3 us
  Pallas kernels  36.6 us (98%)
  between operations  0.64 us (2%)
    pallas_call x1, Pallas kernels, local(): pl.pallas_call(functools.partial(kernel, n, zs), out_shape=(vmem(field.sh...  35.6 us
    pallas_call x1, Pallas kernels, local(): pl.pallas_call(mix, out_shape=(field, field), in_specs=[local_vmem] * 3,...  1.04 us

profile of v4, /device:TPU:1, one launch (start us, length us, event | category | flops | bytes accessed | tf_op | source)
XLA Modules:
  0.0 37.3 jit_solution(12728501883954951860)
XLA Ops:
  0.6 35.6 %shard_map.59 = (f32[32,16,128]{2,1,0:T(8,128)S(1)}, bf16[128,4096]{1,0:T(8,128)(2,1)S(1)}, bf16[64,128]{1,0:T(8,128)(2,1)S(1)}) custom-call(f32[32,16,128]{2,1,0:T(8,128)} %rhs.1, f32[32,5,128,128]{3,2,1,0:T(8,128)} %band.1, f32[1,6,4,128,128]{4,3,2,1,0:T(8,128)} %link.1, s32[1,4,6]{2,1,0:T(4,128)} %bitcast.1), custom_call_target="tpu_custom_call" | custom-call | tf_op jit(solution)/shard_map/pallas_call | solution.py:645
  36.2 1.0 %shard_map.60 = (f32[32,16,128]{2,1,0:T(8,128)}, f32[32,16,128]{2,1,0:T(8,128)}) custom-call(f32[32,16,128]{2,1,0:T(8,128)S(1)} %get-tuple-element.5.v0, bf16[128,4096]{1,0:T(8,128)(2,1)S(1)} %get-tuple-element.6.vs, bf16[64,128]{1,0:T(8,128)(2,1)S(1)} %get-tuple-element.7.mixer), custom_call_target="tpu_custom_call" | custom-call | tf_op jit(solution)/shard_map/pallas_call | solution.py:697

commit v5 on v4

--- a/solution.py
+++ b/solution.py
@@ -120,6 +120,8 @@
     farc,
     mirror1,
     mirror2,
+    own_mean,
+    means,
     sig1,
     sig2,
     gra1,
@@ -134,6 +136,7 @@
     r1,
     s2,
     r2,
+    mean_sem,
 ):
     block_rows = v0.shape[0]
     pairs = block_rows // 2
@@ -273,16 +276,20 @@
             send[step, 0, s] = times_block(0, s, jnp.concatenate(parts, axis=0))
         start_links(step, (0,))
         wait_far(step - 1)
+        for j in (2, 3):
+            for s in range(H):
+                parts = split(row_value(step - 1, own_row(j, s)))
+                send[step, j, s] = times_block(j, s, jnp.concatenate(parts, axis=0))
+        start_links(step, (2, 3))
         each_pair(store)
-        for interfaces in ((2, 3), (4, 5, 1)):
-            multiply_links(step, interfaces)
-            start_links(step, interfaces)
+        multiply_links(step, (4, 5, 1))
+        start_links(step, (4, 5, 1))
 
     def wait_far(step):
         halo_copy(step, 0).wait_recv()
         if step > 0:
             for s in range(H):
-                missing = mirror1[s] if step == 1 else mirror2[s] * (scale * scale)
+                missing = mirror1[s] if step == 1 else mirror2[s] * (ratio * ratio)
                 farc[s + 1] = fars[step][s + 1] + missing
 
     def wait_others(step):
@@ -308,6 +315,26 @@
     with jax.named_scope("links0"):
         load_r.wait()
         multiply_links(0, range(6))
+
+    def mean_copy(j):
+        return pltpu.make_async_remote_copy(
+            src_ref=own_mean,
+            dst_ref=means.at[arrives_at[j]],
+            send_sem=mean_sem.at[0],
+            recv_sem=mean_sem.at[1],
+            device_id=(facing[j],),
+            device_id_type=MESH,
+        )
+
+    def all_means():
+        return pltpu.make_async_remote_copy(
+            src_ref=means,
+            dst_ref=means,
+            send_sem=mean_sem.at[0],
+            recv_sem=mean_sem.at[1],
+            device_id=(facing[1],),
+            device_id_type=MESH,
+        )
 
     def plane_start(which, buffer, value):
         buffer[rank] = value
@@ -428,6 +455,11 @@
         total = lax.fori_loop(0, block_rows, add_diagonal, jnp.zeros((BS, BS), F32), unroll=4)
         mean = jnp.sum(total * (1.0 / (block_rows * BS)), axis=0, keepdims=True)
         plane_start(0, sig1, mean)
+        own = jnp.sum(mean, axis=1, keepdims=True)
+        own_mean[...] = jnp.broadcast_to(own, (1, BS))
+        for j in range(6):
+            mean_copy(j).start()
+        unit = 1.0 / own
 
     lax.fori_loop(ahead, 4, split_chunk, 0)
 
@@ -442,14 +474,13 @@
 
     def row_value(step, g, with_far=True):
         total = yb[g]
-        for j in range(1, 6):
-            total = total + recvs[step][j - 1, inv[g * 6 + j]]
-        if with_far:
-            total = total + (farc if step else far0)[inv[g * 6]]
+        for j in range(0 if with_far else 1, 6):
+            came = recvs[step][j - 1, inv[g * 6 + j]] if j else (farc if step else far0)[inv[g * 6]]
+            total = total + (came * exchange[j] if step == 1 else came)
         if step == 0:
-            return total
+            return total * unit
         if step == 1:
-            return (total * scale - w1[g]) * scale - (w1[g] * scale - v0[g])
+            return (total * scale - w1[g]) * ratio - (w1[g] * ratio - v0[g])
         return total * scale - v2[g]
 
     def pair_value(step, p):
@@ -471,9 +502,12 @@
     with jax.named_scope("sig_ring"):
         ring_start(0, sig2, plane_finish(0, sig1))
     with jax.named_scope("mirror"):
+        all_means().wait_recv()
+        exchange = [means[j] * unit for j in range(6)]
+        theirs = 1.0 / means[0]
         for s in range(H):
-            mirror1[s] = times_transpose(s, send[0, 0, s])
-            mirror2[s] = times_transpose(s, times_block(0, s, vr[own_row(0, s)]))
+            mirror1[s] = times_transpose(s, send[0, 0, s] * theirs)
+            mirror2[s] = times_transpose(s, times_block(0, s, vr[own_row(0, s)]) * unit)
     with jax.named_scope("band1"):
         band_product()
     with jax.named_scope("halo1"):
@@ -481,10 +515,11 @@
     with jax.named_scope("sig_wait"):
         sigma = jnp.sum(ring_finish(0, sig2) * (1.0 / n), axis=1, keepdims=True)
         scale = 1.0 / sigma
+        ratio = own * scale
 
     def store_v2(p):
         first = jnp.concatenate([w1[2 * p], w1[2 * p + 1]], axis=1)
-        keep(p, 1, *split(first * scale - first_field(p)))
+        keep(p, 1, *split(first * ratio - first_field(p)))
         value = pair_value(1, p)
         v2[2 * p], v2[2 * p + 1] = value[:, :BS], value[:, BS:]
         put(p, value, 2)
@@ -548,6 +583,7 @@
     with jax.named_scope("sent"):
         for step in range(3):
             links_sent(step)
+        all_means().wait_send()
         plane_sent(0, sig1)
         ring_sent(0, sig2)
         plane_sent(1, gra1)
@@ -670,6 +706,8 @@
                 vmem((H + 1, S, BS), F32),
                 vmem((H, S, BS), F32),
                 vmem((H, S, BS), F32),
+                vmem((1, BS), F32),
+                vmem((6, 1, BS), F32),
                 vmem((group, 1, BS), F32),
                 vmem((zs, 1, BS), F32),
                 vmem((group, 5, 2, BS), F32),
@@ -684,6 +722,7 @@
                 dma((3,)),
                 dma((3,)),
                 dma((3,)),
+                dma((2,)),
             ],
             compiler_params=pltpu.CompilerParams(
                 collective_id=0, has_side_effects=True, vmem_limit_bytes=62 * 1024 * 1024

time: 37.4 us -> 37.4 us (level)
  no operation moved by 1% of the time
where the time goes in v5:
time: 37.4 us; the launch traced here: 37.3 us
  Pallas kernels  36.6 us (98%)
  between operations  0.64 us (2%)
    pallas_call x1, Pallas kernels, local(): pl.pallas_call(functools.partial(kernel, n, zs), out_shape=(vmem(field.sh...  35.6 us
    pallas_call x1, Pallas kernels, local(): pl.pallas_call(mix, out_shape=(field, field), in_specs=[local_vmem] * 3,...  1.04 us

profile of v5, /device:TPU:1, one launch (start us, length us, event | category | flops | bytes accessed | tf_op | source)
XLA Modules:
  0.0 37.3 jit_solution(11025496492910053617)
XLA Ops:
  0.6 35.6 %shard_map.59 = (f32[32,16,128]{2,1,0:T(8,128)S(1)}, bf16[128,4096]{1,0:T(8,128)(2,1)S(1)}, bf16[64,128]{1,0:T(8,128)(2,1)S(1)}) custom-call(f32[32,16,128]{2,1,0:T(8,128)} %rhs.1, f32[32,5,128,128]{3,2,1,0:T(8,128)} %band.1, f32[1,6,4,128,128]{4,3,2,1,0:T(8,128)} %link.1, s32[1,4,6]{2,1,0:T(4,128)} %bitcast.1), custom_call_target="tpu_custom_call" | custom-call | tf_op jit(solution)/shard_map/pallas_call | solution.py:681
  36.2 1.0 %shard_map.60 = (f32[32,16,128]{2,1,0:T(8,128)}, f32[32,16,128]{2,1,0:T(8,128)}) custom-call(f32[32,16,128]{2,1,0:T(8,128)S(1)} %get-tuple-element.5.v0, bf16[128,4096]{1,0:T(8,128)(2,1)S(1)} %get-tuple-element.6.vs, bf16[64,128]{1,0:T(8,128)(2,1)S(1)} %get-tuple-element.7.mixer), custom_call_target="tpu_custom_call" | custom-call | tf_op jit(solution)/shard_map/pallas_call | solution.py:736

commit v6 on v5

--- a/solution.py
+++ b/solution.py
@@ -143,14 +143,14 @@
     group = n // zs
     me = lax.axis_index("dom")
     core = lax.rem(me, 2)
-    given = (1 - core, core, 2, 3, 4, 5)
+    given = (1 - core, core, 4, 5, 2, 3)
     facing = (
         lax.rem(me + (n - 1) + 2 * core, n),
         me ^ 1,
+        lax.rem(me + n // 4, n),
+        lax.rem(me + (n - n // 4), n),
         lax.rem(me + n // 16, n),
         lax.rem(me + (n - n // 16), n),
-        lax.rem(me + n // 4, n),
-        lax.rem(me + (n - n // 4), n),
     )
     arrives_at = (0, 1, 3, 2, 5, 4)
     z = lax.rem(lax.div(me, 2), zs)
@@ -237,7 +237,6 @@
                 links[j, s, pl.ds(0, BS)] = hi
                 links[j, s, pl.ds(BS, BS)] = lo
 
-    others = pl.ds(1, 5)
     slots = pl.ds(1, H)
     recvs, fars = (recv0, recv1, recv2), (far0, far1, far2)
 
@@ -246,7 +245,7 @@
             src_ref=send.at[step, j],
             dst_ref=recvs[step].at[arrives_at[j] - 1, slots] if j else fars[step].at[slots],
             send_sem=halo_send.at[step],
-            recv_sem=halo_recv.at[step, min(j, 1)],
+            recv_sem=halo_recv.at[step, (0, 1, 1, 1, 2, 2)[j]],
             device_id=(facing[j],),
             device_id_type=MESH,
         )
@@ -276,14 +275,14 @@
             send[step, 0, s] = times_block(0, s, jnp.concatenate(parts, axis=0))
         start_links(step, (0,))
         wait_far(step - 1)
-        for j in (2, 3):
+        for j in (4, 5):
             for s in range(H):
                 parts = split(row_value(step - 1, own_row(j, s)))
                 send[step, j, s] = times_block(j, s, jnp.concatenate(parts, axis=0))
-        start_links(step, (2, 3))
+        start_links(step, (4, 5))
         each_pair(store)
-        multiply_links(step, (4, 5, 1))
-        start_links(step, (4, 5, 1))
+        multiply_links(step, (2, 3, 1))
+        start_links(step, (2, 3, 1))
 
     def wait_far(step):
         halo_copy(step, 0).wait_recv()
@@ -292,15 +291,21 @@
                 missing = mirror1[s] if step == 1 else mirror2[s] * (ratio * ratio)
                 farc[s + 1] = fars[step][s + 1] + missing
 
-    def wait_others(step):
+    def wait_group(step, which):
+        group_of = pl.ds(0, 3) if which == 1 else pl.ds(3, 2)
+        came = recvs[step].at[group_of, slots]
         pltpu.make_async_remote_copy(
-            src_ref=send.at[step, others],
-            dst_ref=recvs[step].at[:, slots],
+            src_ref=came,
+            dst_ref=came,
             send_sem=halo_send.at[step],
-            recv_sem=halo_recv.at[step, 1],
+            recv_sem=halo_recv.at[step, which],
             device_id=(facing[1],),
             device_id_type=MESH,
         ).wait_recv()
+
+    def wait_others(step):
+        wait_group(step, 1)
+        wait_group(step, 2)
 
     def links_sent(step):
         pltpu.make_async_remote_copy(
@@ -562,15 +567,16 @@
         )
 
     with jax.named_scope("halo2"):
-        wait_others(2)
+        wait_group(2, 1)
     with jax.named_scope("gram_o"):
-        came = [recv2[j, s + 1] for j in range(5) for s in range(H)]
-        partial = partial + halves(gram_of_arrived(jnp.concatenate(mine[1:], axis=1), came)) * scale
+        came = [recv2[j, s + 1] for j in range(3) for s in range(H)]
+        partial = partial + halves(gram_of_arrived(jnp.concatenate(mine[1:4], axis=1), came)) * scale
     with jax.named_scope("far2"):
+        wait_group(2, 2)
         wait_far(2)
     with jax.named_scope("gram_c"):
-        came = [farc[s + 1] for s in range(H)]
-        last = partial + halves(gram_of_arrived(mine[0], came)) * scale
+        came = [recv2[j, s + 1] for j in (3, 4) for s in range(H)] + [farc[s + 1] for s in range(H)]
+        last = partial + halves(gram_of_arrived(jnp.concatenate(mine[4:] + mine[:1], axis=1), came)) * scale
         plane_start(2, grb1, pack(last, place))
 
     def store_v3(p):
@@ -717,7 +723,7 @@
                 dma((4,)),
                 dma((4, 2)),
                 dma((3,)),
-                dma((3, 2)),
+                dma((3, 3)),
                 dma((3,)),
                 dma((3,)),
                 dma((3,)),

time: 37.4 us -> 37.2 us (level)
  no operation moved by 1% of the time
where the time goes in v6:
time: 37.2 us; the launch traced here: 37.1 us
  Pallas kernels  36.5 us (98%)
  between operations  0.64 us (2%)
    pallas_call x1, Pallas kernels, local(): pl.pallas_call(functools.partial(kernel, n, zs), out_shape=(vmem(field.sh...  35.4 us
    pallas_call x1, Pallas kernels, local(): pl.pallas_call(mix, out_shape=(field, field), in_specs=[local_vmem] * 3,...  1.04 us

profile of v6, /device:TPU:1, one launch (start us, length us, event | category | flops | bytes accessed | tf_op | source)
XLA Modules:
  0.0 37.1 jit_solution(1693629321683572819)
XLA Ops:
  0.6 35.4 %shard_map.59 = (f32[32,16,128]{2,1,0:T(8,128)S(1)}, bf16[128,4096]{1,0:T(8,128)(2,1)S(1)}, bf16[64,128]{1,0:T(8,128)(2,1)S(1)}) custom-call(f32[32,16,128]{2,1,0:T(8,128)} %rhs.1, f32[32,5,128,128]{3,2,1,0:T(8,128)} %band.1, f32[1,6,4,128,128]{4,3,2,1,0:T(8,128)} %link.1, s32[1,4,6]{2,1,0:T(4,128)} %bitcast.1), custom_call_target="tpu_custom_call" | custom-call | tf_op jit(solution)/shard_map/pallas_call | solution.py:687
  36.1 1.0 %shard_map.60 = (f32[32,16,128]{2,1,0:T(8,128)}, f32[32,16,128]{2,1,0:T(8,128)}) custom-call(f32[32,16,128]{2,1,0:T(8,128)S(1)} %get-tuple-element.5.v0, bf16[128,4096]{1,0:T(8,128)(2,1)S(1)} %get-tuple-element.6.vs, bf16[64,128]{1,0:T(8,128)(2,1)S(1)} %get-tuple-element.7.mixer), custom_call_target="tpu_custom_call" | custom-call | tf_op jit(solution)/shard_map/pallas_call | solution.py:742
